TPU v7x, 32 devices: a whole 2x2x4 slice. The times are simulated.
32 devices in a mesh: expert: 4 (over y, core), mp: 8 (over z, x).
Axes of the slice: x: 2, y: 2, z: 4, core: 2. Of those that a mesh axis runs over, the one named last changes fastest.
Arguments:
- tokens: bfloat16 [512, 6144], P(('expert', 'mp')), may hold values from -18 to 18
- norm_gain: bfloat16 [6144], replicated, may hold values from 0.099609375 to 1.8984375
- expert_ids: int32 [512, 2], P(('expert', 'mp')), may hold values from 0 to 3, as said below
- slot_ids: int32 [512, 2], P(('expert', 'mp')), may hold values from 0 to 7, as said below
- route_weights: float32 [512, 2], P(('expert', 'mp')), may hold values from 0.1 to 1
- w_gate: bfloat16 [4, 6144, 8192], P('expert', None, 'mp'), may hold values from -0.078125 to 0.078125
- w_up: bfloat16 [4, 6144, 8192], P('expert', None, 'mp'), may hold values from -0.078125 to 0.078125
- w_down: bfloat16 [4, 8192, 6144], P('expert', 'mp'), may hold values from -0.0625 to 0.0625
Outputs:
- moe_out: bfloat16 [512, 6144], P(('expert', 'mp'))
Inputs may be any that keep to these rules, and one draw needn't show every extreme that they name: `expert_ids`: each token names two different experts. Among the 16 tokens of one device (aligned blocks of rows) no expert is named more than 8 times, and on every device some expert is named exactly 8 times. `slot_ids`: within the tokens of one device, the entries that name the same expert have different slots; slots that no entry names stay empty.
All inputs are finite; a program needn't handle non-finite values.
Results may differ from a plain program's by a relative error of at most 0.015.
Values may be sent and summed in bfloat16 or wider, within the bound.
No kernel may reach another device: no remote copies, remote signals or barrier semaphores. Data moves between devices by JAX's collectives and lax.ppermute only.
A program may use at most 128 MiB of HBM per device.

v0:
```python
import jax
import jax.numpy as jnp
from jax import lax
from jax.sharding import PartitionSpec as P

CAP = 8


def local(tokens, norm_gain, expert_ids, slot_ids, route_weights, w_gate, w_up, w_down):
    tok_rows = tokens.shape[0]
    features = tokens.shape[1]
    experts = w_gate.shape[0] * lax.axis_size("expert")
    values = tokens.astype(jnp.float32)
    mean_square = jnp.mean(values * values, axis=1, keepdims=True)
    normed = (values * lax.rsqrt(mean_square + 1e-05) * norm_gain.astype(jnp.float32)).astype(
        jnp.bfloat16
    )
    target = expert_ids * CAP + slot_ids
    places = lax.broadcasted_iota(jnp.int32, (experts * CAP, tok_rows, 2), 0)
    placing = jnp.any(places == target[None, :, :], axis=2).astype(jnp.bfloat16)
    outgoing = jnp.dot(placing, normed, preferred_element_type=jnp.float32).astype(jnp.bfloat16)
    outgoing = outgoing.reshape(experts, CAP, features)
    gate_local = w_gate[0]
    up_local = w_up[0]
    down_local = w_down[0]
    arrived = lax.all_to_all(outgoing, "expert", split_axis=0, concat_axis=0, tiled=True)
    piece = lax.all_gather(arrived.reshape(experts * CAP, features), "mp", axis=0, tiled=True)
    gate_proj = jnp.dot(piece, gate_local, preferred_element_type=jnp.float32)
    up_proj = jnp.dot(piece, up_local, preferred_element_type=jnp.float32)
    hidden = (jax.nn.silu(gate_proj) * up_proj).astype(jnp.bfloat16)
    piece = hidden
    summed = lax.psum_scatter(
        jnp.dot(piece, down_local, preferred_element_type=jnp.float32).astype(jnp.bfloat16),
        "mp",
        scatter_dimension=0,
        tiled=True,
    )
    results = summed.reshape(experts, CAP, features)
    returned = lax.all_to_all(results, "expert", split_axis=0, concat_axis=0, tiled=True)
    flattened = returned.reshape(experts * CAP, features)
    picked = flattened[target].astype(jnp.float32)
    shares = route_weights / (route_weights[:, 0:1] + route_weights[:, 1:2])
    mixed = jnp.sum(shares[:, :, None] * picked, axis=1)
    return mixed.astype(jnp.bfloat16)


def solution(mesh):
    placed = (
        P(("expert", "mp"), None),
        P(),
        P(("expert", "mp"), None),
        P(("expert", "mp"), None),
        P(("expert", "mp"), None),
        P("expert", None, "mp"),
        P("expert", None, "mp"),
        P("expert", "mp", None),
    )
    return jax.shard_map(
        local, mesh=mesh, in_specs=placed, out_specs=P(("expert", "mp"), None), check_vma=False
    )
```

profile of v0, /device:TPU:0, one launch (start us, length us, event | category | flops | bytes accessed | tf_op | source)
XLA Modules:
  0.0 203.9 jit_solution(15964575743385824110)
XLA Ops:
  6.5 0.0 all-gather.2.cloned.1.call-start
  6.5 0.7 compare_select_fusion
  7.2 0.1 fusion.22
  7.3 0.7 convert_element_type.26
  8.0 1.1 fusion.16
  9.1 1.2 fusion.9
  10.4 11.6 %all_to_all.10 = bf16[4,8,6144]{2,1,0:T(8,128)(2,1)} all-to-all(bf16[4,8,6144]{2,1,0:T(8,128)(2,1)S(1)} %fusion.9), channel_id=1, replica_groups=mesh['expert'=4,'mp'=8] {'expert'}, dimensions={0} | all-to-all | bytes 786432 | tf_op jit(solution)/shard_map/all_to_all | solution.py:26
  22.0 0.0 all-gather.2.cloned.1.call-update
  22.0 0.0 reduce-scatter.2.cloned.1.call-start
  22.0 60.8 %all-gather.2.cloned.1.call-done = bf16[256,6144]{1,0:T(8,128)(2,1)} async-done(((bf16[32,6144]{1,0:T(8,128)(2,1)}), bf16[256,6144]{1,0:T(8,128)(2,1)}) %all-gather.2.cloned.1.call-update) | async-done | bytes 3145744 | tf_op jit(solution)/shard_map/all_gather | solution.py:27
  82.8 0.0 copy-start.1
  82.8 10.1 %fusion.4 = f32[256,1024]{1,0:T(8,128)} fusion(bf16[256,6144]{1,0:T(8,128)(2,1)} %all-gather.2.cloned.1.call-done, bf16[1,6144,1024]{2,1,0:T(8,128)(2,1)} %param.13), kind=kOutput, calls=%fused_computation.5 | convolution fusion | flops 3221225472 | bytes 16777216 | tf_op jit(solution)/shard_map/dot_general | solution.py:28
  92.9 0.0 copy-done.1
  92.9 0.0 copy-start
  92.9 17.0 %fusion.6 = bf16[256,6144]{1,0:T(8,128)(2,1)} fusion(bf16[1,1024,6144]{2,1,0:T(8,128)(2,1)} %param.15, bf16[256,6144]{1,0:T(8,128)(2,1)S(1)} %copy-done.1, bf16[1,6144,1024]{2,1,0:T(8,128)(2,1)} %param.14, f32[256,1024]{1,0:T(8,128)} %fusion.4), kind=kOutput, calls=%fused_computation.7 | convolution fusion | flops 6445596672 | bytes 32505856 | tf_op jit(solution)/shard_map/dot_general | solution.py:33
  109.9 0.0 reduce-scatter.2.cloned.1.call-update
  109.9 0.1 copy.16
  110.0 0.1 reshape.29
  110.1 0.0 copy-done
  110.1 73.0 %reduce-scatter.2.cloned.1.call-done = bf16[32,6144]{1,0:T(8,128)(2,1)} async-done(((bf16[256,6144]{1,0:T(8,128)(2,1)}), bf16[32,6144]{1,0:T(8,128)(2,1)}) %reduce-scatter.2.cloned.1.call-update) | async-done | bytes 393232 | tf_op jit(solution)/shard_map/reduce_scatter | solution.py:32
  183.1 3.5 %all-to-all-start.1 = ((bf16[4,8,6144]{2,1,0:T(8,128)(2,1)}), bf16[4,8,6144]{2,1,0:T(8,128)(2,1)S(1)}, u32[]{:S(2)}, u32[]{:S(2)}) async-start(bf16[4,8,6144]{2,1,0:T(8,128)(2,1)} %bitcast.36), calls=%async_computation.2 | async-start | bytes 786432 | tf_op jit(solution)/shard_map/all_to_all | solution.py:39
  186.6 0.1 copy.15
  186.7 7.3 %all-to-all-done.1 = bf16[4,8,6144]{2,1,0:T(8,128)(2,1)S(1)} async-done(((bf16[4,8,6144]{2,1,0:T(8,128)(2,1)}), bf16[4,8,6144]{2,1,0:T(8,128)(2,1)S(1)}, u32[]{:S(2)}, u32[]{:S(2)}) %all-to-all-start.1) | async-done | bytes 393248 | tf_op jit(solution)/shard_map/all_to_all | solution.py:39
  194.0 0.8 gather_fusion
  194.8 0.5 reshape.37
  195.3 1.7 multiply_reduce_fusion
  (4 shorter events, 0.0 us)
Async XLA Ops:
  6.5 76.3 %all-gather.2.cloned.1.call-start = ((), (), s32[]{:S(2)}) async-start(), calls=%async_computation.3 | async-start | bytes 3538944 | tf_op jit(solution)/shard_map/all_gather | solution.py:27
  22.0 161.2 %reduce-scatter.2.cloned.1.call-start = ((), (), s32[]{:S(2)}) async-start(), calls=%async_computation.4 | async-start | bytes 3538944 | tf_op jit(solution)/shard_map/reduce_scatter | solution.py:32
  82.8 10.1 %copy-start.1 = (bf16[256,6144]{1,0:T(8,128)(2,1)S(1)}, bf16[256,6144]{1,0:T(8,128)(2,1)}, u32[]{:S(2)}) copy-start(bf16[256,6144]{1,0:T(8,128)(2,1)} %all-gather.2.cloned.1.call-done) | copy-start | bytes 9437188
  92.9 17.2 %copy-start = (f32[16,2]{0,1:T(2,128)S(1)}, f32[16,2]{0,1:T(2,128)}, u32[]{:S(2)}) copy-start(f32[16,2]{0,1:T(2,128)} %param.12) | copy-start | bytes 388
  183.1 10.8 %all-to-all-start.1 = ((bf16[4,8,6144]{2,1,0:T(8,128)(2,1)}), bf16[4,8,6144]{2,1,0:T(8,128)(2,1)S(1)}, u32[]{:S(2)}, u32[]{:S(2)}) async-start(bf16[4,8,6144]{2,1,0:T(8,128)(2,1)} %bitcast.36), calls=%async_computation.2 | async-start | bytes 786432 | tf_op jit(solution)/shard_map/all_to_all | solution.py:39
Sparse Core Ops, SparseCore 0:
  22.1 60.6 all-gather.1
  110.1 73.0 reduce-scatter.1
where the time goes:
time: 204 us
  waiting for transfers between devices  141 us (69%)
  matrix products  28.3 us (14%)
  between operations  13.5 us (7%)
  blocking collectives  11.6 us (6%)
  other arithmetic  4.34 us (2%)
  starting transfers between devices  3.5 us (2%)
    reduce_scatter x1, waiting for transfers between devices, local(): lax.psum_scatter(jnp.dot(piece, down_local, preferred_element_type=jnp.fl...  73 us
    all_gather x1, waiting for transfers between devices, local(): lax.all_gather(arrived.reshape(experts * CAP, features), 'mp', axis=0, ti...  60.8 us
    dot_general x1, matrix products, local(): jnp.dot(piece, down_local, preferred_element_type=jnp.float32)  17 us
    all_to_all x1, blocking collectives, local(): lax.all_to_all(outgoing, 'expert', split_axis=0, concat_axis=0, tiled=True)  11.6 us
    dot_general x1, matrix products, local(): gate_proj = jnp.dot(piece, gate_local, preferred_element_type=jnp.float32)  10.1 us
    all_to_all x1, waiting for transfers between devices, local(): lax.all_to_all(results, 'expert', split_axis=0, concat_axis=0, tiled=True)  7.27 us
  transfers between devices with their start and end apart: 3, of which 3 were waited for; matrix products, arithmetic and copies ran while one was open for 0% of the time, Pallas kernels for 0%

commit v1 on v0

v1 whole, which is shorter than its diff:
```python
import functools

import jax
import jax.numpy as jnp
from jax import lax
from jax.experimental import pallas as pl
from jax.experimental.pallas import tpu as pltpu
from jax.sharding import PartitionSpec as P


CAP = 8
META = 128
FFT = 256
OUT = 1024
PLACE = 2048
MIX = 2048
FFN_VMEM = 32 * 2**20
AXES = ("expert", "mp")


class Grid:
    def __init__(self, sizes):
        self.cores = 2
        self.y = sizes["expert"] // self.cores
        self.x = self.y if sizes["mp"] % self.y == 0 else 1
        self.z = sizes["mp"] // self.x

    def index(self, y, c, z, x):
        return ((y * self.cores + c) * self.z + z) * self.x + x

    def move(self, value, to):
        pairs = []
        for y in range(self.y):
            for c in range(self.cores):
                for z in range(self.z):
                    for x in range(self.x):
                        target = to(y, c, z, x)
                        if target is not None:
                            pairs.append((self.index(y, c, z, x), self.index(*target)))
        return lax.ppermute(value, AXES, pairs)

    def first(self, k):
        return lambda y, c, z, x: (
            (y, c, z, (x + k) % self.x) if c == 0 else ((y + k) % self.y, c, z, x)
        )

    def second(self, k):
        return lambda y, c, z, x: (
            ((y + k) % self.y, c, z, x) if c == 0 else (y, c, z, (x + k) % self.x)
        )

    def sibling(self, y, c, z, x):
        return (y, 1 - c, z, x)

    def across_z(self, k, sign=1):
        if self.z & (self.z - 1) == 0:
            return lambda y, c, z, x: (y, c, z ^ k, x)
        return lambda y, c, z, x: (y, c, (z + sign * k) % self.z, x)


def gather_z(grid, own):
    blocks = [own] + [None] * (grid.z - 1)
    for k in reversed(range(1, grid.z)):
        blocks[k] = grid.move(own, grid.across_z(k))
    return blocks


def scatter_z(grid, parts):
    total = parts[0].astype(jnp.float32)
    for k in range(1, grid.z):
        moved = grid.move(parts[k], grid.across_z(k, -1))
        total = total + moved.astype(jnp.float32)
    return total.astype(jnp.bfloat16)


def spread(grid, block):
    firsts = [block] + [grid.move(block, grid.first(k)) for k in range(1, grid.x)]
    half = jnp.concatenate(firsts, axis=0)
    seconds = [half] + [grid.move(half, grid.second(k)) for k in range(1, grid.y)]
    return jnp.concatenate(seconds, axis=0)


def fold(grid, rows):
    size = rows.shape[0] // grid.y
    moved = [grid.move(rows[k * size : (k + 1) * size], grid.second(-k)) for k in range(1, grid.y)]
    half = sum(moved, rows[:size])
    size = size // grid.x
    moved = [grid.move(half[k * size : (k + 1) * size], grid.first(-k)) for k in range(1, grid.x)]
    return sum(moved, half[:size])


def prepare_kernel(tok_ref, gain_ref, ids_ref, slots_ref, route_ref, out_ref):
    f32, bf16 = jnp.float32, jnp.bfloat16
    _, features = tok_ref.shape
    values = tok_ref[...].astype(f32)
    mean_square = jnp.mean(values * values, axis=1, keepdims=True)
    scale = lax.rsqrt(mean_square + 1e-05)
    for at in range(gain_ref.shape[0]):
        place = slice(at * 128, (at + 1) * 128)
        gain = gain_ref[at : at + 1, :].astype(f32)
        out_ref[:, place] = (values[:, place] * scale * gain).astype(bf16)
    target = (ids_ref[...] * CAP + slots_ref[...]).astype(f32)
    route = route_ref[...]
    shares = route / (route[0:1] + route[1:2])
    high = shares.astype(bf16).astype(f32)
    middle = (shares - high).astype(bf16).astype(f32)
    low = shares - high - middle
    parts = jnp.concatenate([target, high, middle, low], axis=0).astype(bf16)
    row = lax.broadcasted_iota(jnp.int32, (parts.shape[0], META), 0)
    lane = lax.broadcasted_iota(jnp.int32, (parts.shape[0], META), 1)
    select = (row == lane).astype(bf16)
    turned = lax.dot_general(
        parts, select, (((0,), (0,)), ((), ())), preferred_element_type=f32
    )
    out_ref[:, features:] = turned.astype(bf16)


def prepare(tokens, norm_gain, expert_ids, slot_ids, route_weights):
    rows, features = tokens.shape
    return pl.pallas_call(
        prepare_kernel,
        out_shape=jax.ShapeDtypeStruct((rows, features + META), jnp.bfloat16),
        name="prepare",
    )(tokens, norm_gain.reshape(-1, 128), expert_ids.T, slot_ids.T, route_weights.T)


def hits(metas, expert, tok_rows, cores):
    meta = jnp.concatenate(metas, axis=0).astype(jnp.float32)
    count = meta.shape[0]
    each = count // tok_rows * CAP
    block = lax.broadcasted_iota(jnp.int32, (count, 2), 0) // tok_rows * CAP
    places = jnp.full((count, 2), -1.0, jnp.float32)
    for side in range(cores):
        first = ((expert ^ side) * CAP).astype(jnp.float32)
        slots = meta[:, 0:2] - first
        here = (slots >= 0) & (slots < CAP)
        places = jnp.where(here, slots + (block + side * each).astype(jnp.float32), places)
    index = lax.broadcasted_iota(jnp.int32, (count, cores * each), 1).astype(jnp.float32)
    share = meta[:, 2:4] + meta[:, 4:6] + meta[:, 6:8]
    return [index == places[:, k : k + 1] for k in range(2)], share


def place_kernel(n, tok_rows, features, *refs):
    f32, bf16 = jnp.float32, jnp.bfloat16
    blocks, outs = refs[:n], refs[n:]
    expert = lax.axis_index("expert")
    hit, _ = hits([b[:, features:] for b in blocks], expert, tok_rows, len(outs))
    placing = (hit[0] | hit[1]).astype(f32).T.astype(bf16)
    each = outs[0].shape[0]

    @pl.loop(0, features // PLACE)
    def _(j):
        place = pl.ds(pl.multiple_of(j * PLACE, PLACE), PLACE)
        known = jnp.concatenate([b[:, place] for b in blocks], axis=0)
        got = jnp.dot(placing, known, preferred_element_type=f32).astype(bf16)
        for side, out in enumerate(outs):
            out[:, place] = got[side * each : (side + 1) * each]


def place_rows(groups, tok_rows, features):
    count = sum(g.shape[0] for g in groups)
    each = count // tok_rows * CAP
    vmem = pl.BlockSpec(memory_space=pltpu.VMEM)
    out = jax.ShapeDtypeStruct((each, features), jnp.bfloat16)
    return pl.pallas_call(
        functools.partial(place_kernel, len(groups), tok_rows, features),
        out_shape=[out] * 2,
        in_specs=[vmem] * len(groups),
        out_specs=[vmem] * 2,
        cost_estimate=pl.CostEstimate(
            flops=4 * count * each * features, bytes_accessed=4 * count * features, transcendentals=0
        ),
        compiler_params=pltpu.CompilerParams(vmem_limit_bytes=count * 28 * 2**10),
        name="place",
    )(*groups)


def ffn_kernel(features, mine, theirs, gate, up_hbm, down_hbm, out_mine, out_theirs, *scratch):
    f32, bf16 = jnp.float32, jnp.bfloat16
    up, down, gated, hidden, up_sems, down_sems = scratch
    width, each = gate.shape[2], mine.shape[0]
    up_tiles, down_tiles = width // FFT, features // OUT

    def piece():
        return jnp.concatenate([mine[...], theirs[...]], axis=0)

    def tile(i, size):
        return pl.ds(pl.multiple_of(i * size, size), size)

    def up_copy(i):
        place = tile(i, FFT)
        return pltpu.make_async_copy(up_hbm.at[0, :, place], up.at[:, place], up_sems.at[i])

    def down_copy(i):
        place = tile(i, OUT)
        return pltpu.make_async_copy(down_hbm.at[0, :, place], down.at[:, place], down_sems.at[i])

    for i in range(up_tiles):
        up_copy(i).start()

    @pl.loop(0, up_tiles)
    def _(i):
        gate_proj = jnp.dot(piece(), gate[0, :, tile(i, FFT)], preferred_element_type=f32)
        gated[:, tile(i, FFT)] = gate_proj / (1.0 + jnp.exp(-gate_proj))

    for i in range(down_tiles):
        down_copy(i).start()

    @pl.loop(0, up_tiles)
    def _(i):
        up_copy(i).wait()
        up_proj = jnp.dot(piece(), up[:, tile(i, FFT)], preferred_element_type=f32)
        hidden[:, tile(i, FFT)] = (gated[:, tile(i, FFT)] * up_proj).astype(bf16)

    @pl.loop(0, down_tiles)
    def _(i):
        down_copy(i).wait()
        place = tile(i, OUT)
        product = jnp.dot(hidden[...], down[:, place], preferred_element_type=f32)
        product = product.astype(bf16)
        out_mine[:, place] = product[:each]
        out_theirs[:, place] = product[each:]


def ffn(mine, theirs, w_gate, w_up, w_down):
    bf16 = jnp.bfloat16
    each, features = mine.shape
    width = w_gate.shape[2]
    need = 2 * (3 * features * width + 4 * each * features + 2 * each * width)
    if need > 56 * 2**20 or width % FFT or features % OUT:
        piece = jnp.concatenate([mine, theirs], axis=0)
        gate_proj = jnp.dot(piece, w_gate[0], preferred_element_type=jnp.float32)
        up_proj = jnp.dot(piece, w_up[0], preferred_element_type=jnp.float32)
        hidden = (jax.nn.silu(gate_proj) * up_proj).astype(bf16)
        product = jnp.dot(hidden, w_down[0], preferred_element_type=jnp.float32).astype(bf16)
        return product[:each], product[each:]
    vmem, hbm = pl.BlockSpec(memory_space=pltpu.VMEM), pl.BlockSpec(memory_space=pltpu.HBM)
    return pl.pallas_call(
        functools.partial(ffn_kernel, features),
        out_shape=[jax.ShapeDtypeStruct(mine.shape, bf16)] * 2,
        in_specs=[vmem] * 3 + [hbm] * 2,
        out_specs=[vmem] * 2,
        scratch_shapes=[
            pltpu.VMEM((features, width), bf16),
            pltpu.VMEM((width, features), bf16),
            pltpu.VMEM((2 * each, width), jnp.float32),
            pltpu.VMEM((2 * each, width), bf16),
            pltpu.SemaphoreType.DMA((width // FFT,)),
            pltpu.SemaphoreType.DMA((features // OUT,)),
        ],
        cost_estimate=pl.CostEstimate(
            flops=12 * each * features * width,
            bytes_accessed=6 * features * width,
            transcendentals=2 * each * width,
        ),
        compiler_params=pltpu.CompilerParams(vmem_limit_bytes=FFN_VMEM),
        name="ffn",
    )(mine, theirs, w_gate, w_up, w_down)


def mix_kernel(n, tok_rows, features, *refs):
    f32, bf16 = jnp.float32, jnp.bfloat16
    metas, (mine, theirs), outs = refs[:n], refs[n : n + 2], refs[n + 2 :]
    expert = lax.axis_index("expert")
    hit, share = hits([m[...] for m in metas], expert, tok_rows, 2)
    taking = [h.astype(f32).astype(bf16) for h in hit]

    @pl.loop(0, features // MIX)
    def _(j):
        place = pl.ds(pl.multiple_of(j * MIX, MIX), MIX)
        product = jnp.concatenate([mine[:, place], theirs[:, place]], axis=0)
        total = share[:, 0:1] * jnp.dot(taking[0], product, preferred_element_type=f32)
        total += share[:, 1:2] * jnp.dot(taking[1], product, preferred_element_type=f32)
        total = total.astype(bf16)
        at = 0
        for out in outs:
            out[:, place] = total[at : at + out.shape[0]]
            at += out.shape[0]


def mix(groups, mine, theirs, tok_rows):
    features = mine.shape[1]
    n = len(groups)
    vmem = pl.BlockSpec(memory_space=pltpu.VMEM)
    last = features // META
    metas = [
        pl.BlockSpec((g.shape[0], META), lambda i: (0, last), memory_space=pltpu.VMEM) for g in groups
    ]
    whole = pl.BlockSpec(mine.shape, lambda i: (0, 0))
    count = sum(g.shape[0] for g in groups)
    return pl.pallas_call(
        functools.partial(mix_kernel, n, tok_rows, features),
        grid=(1,),
        out_shape=[jax.ShapeDtypeStruct((g.shape[0], features), jnp.bfloat16) for g in groups],
        in_specs=metas + [whole] * 2,
        out_specs=[pl.BlockSpec((g.shape[0], features), lambda i: (0, 0)) for g in groups],
        cost_estimate=pl.CostEstimate(
            flops=8 * count * mine.shape[0] * features,
            bytes_accessed=4 * count * features,
            transcendentals=0,
        ),
        compiler_params=pltpu.CompilerParams(vmem_limit_bytes=count * 28 * 2**10),
        name="mix",
    )(*groups, mine, theirs)


def local(grid, tokens, norm_gain, expert_ids, slot_ids, route_weights, w_gate, w_up, w_down):
    tok_rows, features = tokens.shape
    own = prepare(tokens, norm_gain, expert_ids, slot_ids, route_weights)
    groups = [spread(grid, block) for block in gather_z(grid, own)]
    mine, away = place_rows(groups, tok_rows, features)
    theirs = grid.move(away, grid.sibling)
    mine, away = ffn(mine, theirs, w_gate, w_up, w_down)
    theirs = grid.move(away, grid.sibling)
    parts = list(mix(groups, mine, theirs, tok_rows))
    for k in reversed(range(grid.z)):
        parts[k] = fold(grid, parts[k])
    return scatter_z(grid, parts)


def solution(mesh):
    grid = Grid(mesh.shape)
    placed = (
        P(("expert", "mp"), None),
        P(),
        P(("expert", "mp"), None),
        P(("expert", "mp"), None),
        P(("expert", "mp"), None),
        P("expert", None, "mp"),
        P("expert", None, "mp"),
        P("expert", "mp", None),
    )

    def body(*args):
        return local(grid, *args)

    return jax.shard_map(
        body, mesh=mesh, in_specs=placed, out_specs=P(("expert", "mp"), None), check_vma=False
    )
```

time: 204 us -> 115 us (0.56)
  waiting for transfers between devices: 141 us -> 62.9 us
  matrix products: 28.3 us -> 0 us
  starting transfers between devices: 3.5 us -> 29.6 us
  Pallas kernels: 0 us -> 18.6 us
  between operations: 13.5 us -> 0.21 us
  blocking collectives: 11.6 us -> 0 us
    reduce_scatter x1 -> x0, waiting for transfers between devices: 73 us -> none  [local(): lax.psum_scatter(jnp.dot(piece, down_local, preferred_element_type=jnp.fl...]
    ppermute x0 -> x24, waiting for transfers between devices: none -> 62.9 us  [move(): return lax.ppermute(value, AXES, pairs)]
    all_gather x1 -> x0, waiting for transfers between devices: 60.8 us -> none  [local(): lax.all_gather(arrived.reshape(experts * CAP, features), 'mp', axis=0, ti...]
    ppermute x0 -> x24, starting transfers between devices: none -> 29.6 us  [move(): return lax.ppermute(value, AXES, pairs)]
    dot_general x3 -> x0, matrix products: 28.3 us -> none  [the longest x1 17 us: local(): jnp.dot(piece, down_local, preferred_element_type=jnp.float32)]
    pallas_call x0 -> x4, Pallas kernels: none -> 18.6 us  [the longest x1 12.8 us: ffn(): pl.pallas_call(functools.partial(ffn_kernel, features), out_shape=[jax.Sh...]
    all_to_all x1 -> x0, blocking collectives: 11.6 us -> none  [local(): lax.all_to_all(outgoing, 'expert', split_axis=0, concat_axis=0, tiled=True)]
    all_to_all x1 -> x0, waiting for transfers between devices: 7.27 us -> none  [local(): lax.all_to_all(results, 'expert', split_axis=0, concat_axis=0, tiled=True)]
  transfers between devices with their start and end apart: 3 -> 24, of which waited for: 3 -> 14; matrix products, arithmetic and copies ran while one was open for 0% -> 2% of each run, Pallas kernels for 0% -> 0%
where the time goes in v1:
time: 115 us
  waiting for transfers between devices  62.9 us (55%)
  starting transfers between devices  29.6 us (26%)
  Pallas kernels  18.6 us (16%)
  other arithmetic  3.3 us (3%)
    ppermute x24, waiting for transfers between devices, move(): return lax.ppermute(value, AXES, pairs)  62.9 us
    ppermute x24, starting transfers between devices, move(): return lax.ppermute(value, AXES, pairs)  29.6 us
    pallas_call x1, Pallas kernels, ffn(): pl.pallas_call(functools.partial(ffn_kernel, features), out_shape=[jax.Sh...  12.8 us
    pallas_call x1, Pallas kernels, mix(): pl.pallas_call(functools.partial(mix_kernel, n, tok_rows, features), grid...  2.38 us
  transfers between devices with their start and end apart: 24, of which 14 were waited for; matrix products, arithmetic and copies ran while one was open for 2% of the time, Pallas kernels for 0%

profile of v1, /device:TPU:0, one launch (start us, length us, event | category | flops | bytes accessed | tf_op | source)
XLA Modules:
  0.0 115.0 jit_solution(11903656640136936308)
XLA Ops:
  0.0 1.8 %prepare.1 = bf16[16,6272]{1,0:T(8,128)(2,1)} custom-call(bf16[16,6144]{1,0:T(8,128)(2,1)} %tok_ref.1, bf16[48,128]{1,0:T(8,128)(2,1)} %bitcast.4, s32[2,16]{1,0:T(2,128)} %bitcast.5, s32[2,16]{1,0:T(2,128)} %bitcast.6, f32[2,16]{1,0:T(2,128)} %bitcast.7), custom_call_target="tpu_custom_call" | custom-call | tf_op jit(solution)/shard_map/prepare/pallas_call | solution.py:120
  1.8 3.0 %collective-permute-start = (bf16[16,6272]{1,0:T(8,128)(2,1)}, bf16[16,6272]{1,0:T(8,128)(2,1)S(1)}, u32[]{:S(2)}, u32[]{:S(2)}) collective-permute-start(bf16[16,6272]{1,0:T(8,128)(2,1)} %prepare.1), channel_id=1, source_target_pairs={{0,1},{1,0},{2,3},{3,2},{4,5},{5,4},{6,7},{7,6},{8,24},{9,25},{10,... | collective-permute-start | bytes 602120 | tf_op jit(solution)/shard_map/ppermute | solution.py:40
  4.8 3.6 %collective-permute-start.8 = (bf16[16,6272]{1,0:T(8,128)(2,1)}, bf16[16,6272]{1,0:T(8,128)(2,1)S(1)}, u32[]{:S(2)}, u32[]{:S(2)}) collective-permute-start(bf16[16,6272]{1,0:T(8,128)(2,1)} %prepare.1), channel_id=1, source_target_pairs={{0,6},{1,7},{2,4},{3,5},{4,2},{5,3},{6,0},{7,1},{8,14},{9,15},{10,... | collective-permute-start | bytes 602120 | tf_op jit(solution)/shard_map/ppermute | solution.py:40
  8.4 0.8 collective-permute-start.2
  9.2 1.1 pad_maximum_fusion.1
  10.3 1.6 %collective-permute-start.1 = (bf16[32,6272]{1,0:T(8,128)(2,1)S(1)}, bf16[32,6272]{1,0:T(8,128)(2,1)S(1)}, u32[]{:S(2)}, u32[]{:S(2)}) collective-permute-start(bf16[32,6272]{1,0:T(8,128)(2,1)S(1)} %pad_maximum_fusion.1), channel_id=1, source_target_pairs={{0,16},{1,17},{2,18},{3,19},{4,20},{5,21},{6,22},{7,23},{8,9},{9,8... | collective-permute-start | bytes 1204232 | tf_op jit(solution)/shard_map/ppermute | solution.py:40
  11.9 2.8 %collective-permute-done.8 = bf16[16,6272]{1,0:T(8,128)(2,1)S(1)} collective-permute-done((bf16[16,6272]{1,0:T(8,128)(2,1)}, bf16[16,6272]{1,0:T(8,128)(2,1)S(1)}, u32[]{:S(2)}, u32[]{:S(2)}) %collective-permute-start.8) | collective-permute-done | bytes 200736 | tf_op jit(solution)/shard_map/ppermute | solution.py:40
  14.8 0.4 collective-permute-start.9
  15.2 10.2 %collective-permute-done.5 = bf16[16,6272]{1,0:T(8,128)(2,1)S(1)} collective-permute-done((bf16[16,6272]{1,0:T(8,128)(2,1)}, bf16[16,6272]{1,0:T(8,128)(2,1)S(1)}, u32[]{:S(2)}, u32[]{:S(2)}) %collective-permute-start.5) | collective-permute-done | bytes 200736 | tf_op jit(solution)/shard_map/ppermute | solution.py:40
  25.4 1.5 %collective-permute-start.6 = (bf16[16,6272]{1,0:T(8,128)(2,1)S(1)}, bf16[16,6272]{1,0:T(8,128)(2,1)S(1)}, u32[]{:S(2)}, u32[]{:S(2)}) collective-permute-start(bf16[16,6272]{1,0:T(8,128)(2,1)S(1)} %collective-permute-done.5), channel_id=1, source_target_pairs={{0,1},{1,0},{2,3},{3,2},{4,5},{5,4},{6,7},{7,6},{8,24},{9,25},{10,... | collective-permute-start | bytes 602120 | tf_op jit(solution)/shard_map/ppermute | solution.py:40
  26.9 0.6 collective-permute-start.3
  27.6 0.6 collective-permute-start.10
  28.2 5.0 %collective-permute-done.6 = bf16[16,6272]{1,0:T(8,128)(2,1)S(1)} collective-permute-done((bf16[16,6272]{1,0:T(8,128)(2,1)S(1)}, bf16[16,6272]{1,0:T(8,128)(2,1)S(1)}, u32[]{:S(2)}, u32[]{:S(2)}) %collective-permute-start.6) | collective-permute-done | bytes 200736 | tf_op jit(solution)/shard_map/ppermute | solution.py:40
  33.1 0.7 collective-permute-start.7
  33.9 3.5 %collective-permute-done.3 = bf16[16,6272]{1,0:T(8,128)(2,1)S(1)} collective-permute-done((bf16[16,6272]{1,0:T(8,128)(2,1)S(1)}, bf16[16,6272]{1,0:T(8,128)(2,1)S(1)}, u32[]{:S(2)}, u32[]{:S(2)}) %collective-permute-start.3) | collective-permute-done | bytes 200736 | tf_op jit(solution)/shard_map/ppermute | solution.py:40
  37.5 0.7 collective-permute-start.4
  38.3 1.0 pad_maximum_fusion.refs_0_
  39.3 1.8 %collective-permute-done.7 = bf16[32,6272]{1,0:T(8,128)(2,1)S(1)} collective-permute-done((bf16[32,6272]{1,0:T(8,128)(2,1)S(1)}, bf16[32,6272]{1,0:T(8,128)(2,1)S(1)}, u32[]{:S(2)}, u32[]{:S(2)}) %collective-permute-start.7) | collective-permute-done | bytes 401440 | tf_op jit(solution)/shard_map/ppermute | solution.py:40
  41.1 4.3 %collective-permute-done.4 = bf16[32,6272]{1,0:T(8,128)(2,1)S(1)} collective-permute-done((bf16[32,6272]{1,0:T(8,128)(2,1)S(1)}, bf16[32,6272]{1,0:T(8,128)(2,1)S(1)}, u32[]{:S(2)}, u32[]{:S(2)}) %collective-permute-start.4) | collective-permute-done | bytes 401440 | tf_op jit(solution)/shard_map/ppermute | solution.py:40
  45.4 1.6 %place.1 = (bf16[128,6144]{1,0:T(8,128)(2,1)S(1)}, bf16[128,6144]{1,0:T(8,128)(2,1)S(1)}) custom-call(bf16[64,6272]{1,0:T(8,128)(2,1)S(1)} %pad_maximum_fusion.refs_0_, bf16[64,6272]{1,0:T(8,128)(2,1)S(1)} %constant_dynamic-update-slice_fusion.refs_1_, bf16[64,6272]{1,0:T(8,128)(2,1)S(1)} %constant_dynamic-update-slice_fusion.3.refs_2_, ...), custom_call_target="tpu_custom_call" | custom-call | flops 805306368 | bytes 6291456 | tf_op jit(solution)/shard_map/place/pallas_call | solution.py:165
  47.0 0.7 collective-permute-start.11
  47.7 3.0 %collective-permute-done.11.theirs = bf16[128,6144]{1,0:T(8,128)(2,1)S(1)} collective-permute-done((bf16[128,6144]{1,0:T(8,128)(2,1)S(1)}, bf16[128,6144]{1,0:T(8,128)(2,1)S(1)}, u32[]{:S(2)}, u32[]{:S(2)}) %collective-permute-start.11) | collective-permute-done | bytes 1572896 | tf_op jit(solution)/shard_map/ppermute | solution.py:40
  50.7 12.8 %ffn.1 = (bf16[128,6144]{1,0:T(8,128)(2,1)S(1)}, bf16[128,6144]{1,0:T(8,128)(2,1)S(1)}) custom-call(bf16[128,6144]{1,0:T(8,128)(2,1)S(1)} %get-tuple-element.13.mine, bf16[128,6144]{1,0:T(8,128)(2,1)S(1)} %collective-permute-done.11.theirs, bf16[1,6144,1024]{2,1,0:T(8,128)(2,1)S(1)} %copy-done, bf16[1,6144,1024]{2,1,0:T(8,128)(2,1)} %up_hbm.1, ...), custom_call_target="tpu_custom_call" | custom-call | flops 9663676416 | bytes 37748736 | tf_op jit(solution)/shard_map/ffn/pallas_call | solution.py:238
  63.5 0.4 collective-permute-start.12
  64.0 3.0 %collective-permute-done.12.refs_5_ = bf16[128,6144]{1,0:T(8,128)(2,1)S(1)} collective-permute-done((bf16[128,6144]{1,0:T(8,128)(2,1)S(1)}, bf16[128,6144]{1,0:T(8,128)(2,1)S(1)}, u32[]{:S(2)}, u32[]{:S(2)}) %collective-permute-start.12) | collective-permute-done | bytes 1572896 | tf_op jit(solution)/shard_map/ppermute | solution.py:40
  67.0 2.4 %mix.1 = (bf16[64,6144]{1,0:T(8,128)(2,1)S(1)}, bf16[64,6144]{1,0:T(8,128)(2,1)S(1)}, bf16[64,6144]{1,0:T(8,128)(2,1)S(1)}, bf16[64,6144]{1,0:T(8,128)(2,1)S(1)}) custom-call(bf16[64,6272]{1,0:T(8,128)(2,1)S(1)} %pad_maximum_fusion.refs_0_, bf16[64,6272]{1,0:T(8,128)(2,1)S(1)} %constant_dynamic-update-slice_fusion.refs_1_, ...), custom_call_target="tpu_custom_call" | custom-call | flops 1610612736 | bytes 6291456 | tf_op jit(solution)/shard_map/mix/pallas_call | solution.py:291
  69.4 0.5 collective-permute-start.21
  70.1 1.6 %collective-permute-start.18 = (bf16[32,6144]{1,0:T(8,128)(2,1)S(1)}, bf16[32,6144]{1,0:T(8,128)(2,1)S(1)}, u32[]{:S(2)}, u32[]{:S(2)}) collective-permute-start(bf16[32,6144]{1,0:T(8,128)(2,1)S(1)} %slice.57), channel_id=1, source_target_pairs={{0,16},{1,17},{2,18},{3,19},{4,20},{5,21},{6,22},{7,23},{8,9},{9,8... | collective-permute-start | bytes 1179656 | tf_op jit(solution)/shard_map/ppermute | solution.py:40
  71.7 0.5 collective-permute-start.15
  72.2 1.6 %collective-permute-start.13 = (bf16[32,6144]{1,0:T(8,128)(2,1)S(1)}, bf16[32,6144]{1,0:T(8,128)(2,1)S(1)}, u32[]{:S(2)}, u32[]{:S(2)}) collective-permute-start(bf16[32,6144]{1,0:T(8,128)(2,1)S(1)} %slice.49), channel_id=1, source_target_pairs={{0,16},{1,17},{2,18},{3,19},{4,20},{5,21},{6,22},{7,23},{8,9},{9,8... | collective-permute-start | bytes 1179656 | tf_op jit(solution)/shard_map/ppermute | solution.py:40
  73.7 3.6 %collective-permute-done.21 = bf16[32,6144]{1,0:T(8,128)(2,1)S(1)} collective-permute-done((bf16[32,6144]{1,0:T(8,128)(2,1)S(1)}, bf16[32,6144]{1,0:T(8,128)(2,1)S(1)}, u32[]{:S(2)}, u32[]{:S(2)}) %collective-permute-start.21) | collective-permute-done | bytes 393248 | tf_op jit(solution)/shard_map/ppermute | solution.py:40
  77.3 0.1 slice_add_fusion
  77.4 1.6 %collective-permute-start.22 = (bf16[16,6144]{1,0:T(8,128)(2,1)S(1)}, bf16[16,6144]{1,0:T(8,128)(2,1)S(1)}, u32[]{:S(2)}, u32[]{:S(2)}) collective-permute-start(bf16[16,6144]{1,0:T(8,128)(2,1)S(1)} %slice.71), channel_id=1, source_target_pairs={{0,1},{1,0},{2,3},{3,2},{4,5},{5,4},{6,7},{7,6},{8,24},{9,25},{10,... | collective-permute-start | bytes 589832 | tf_op jit(solution)/shard_map/ppermute | solution.py:40
  78.9 4.5 %collective-permute-done.18 = bf16[32,6144]{1,0:T(8,128)(2,1)S(1)} collective-permute-done((bf16[32,6144]{1,0:T(8,128)(2,1)S(1)}, bf16[32,6144]{1,0:T(8,128)(2,1)S(1)}, u32[]{:S(2)}, u32[]{:S(2)}) %collective-permute-start.18) | collective-permute-done | bytes 393248 | tf_op jit(solution)/shard_map/ppermute | solution.py:40
  83.4 0.1 slice_add_fusion.1
  83.5 1.6 %collective-permute-start.19 = (bf16[16,6144]{1,0:T(8,128)(2,1)S(1)}, bf16[16,6144]{1,0:T(8,128)(2,1)S(1)}, u32[]{:S(2)}, u32[]{:S(2)}) collective-permute-start(bf16[16,6144]{1,0:T(8,128)(2,1)S(1)} %slice.69), channel_id=1, source_target_pairs={{0,1},{1,0},{2,3},{3,2},{4,5},{5,4},{6,7},{7,6},{8,24},{9,25},{10,... | collective-permute-start | bytes 589832 | tf_op jit(solution)/shard_map/ppermute | solution.py:40
  85.1 4.8 %collective-permute-done.15 = bf16[32,6144]{1,0:T(8,128)(2,1)S(1)} collective-permute-done((bf16[32,6144]{1,0:T(8,128)(2,1)S(1)}, bf16[32,6144]{1,0:T(8,128)(2,1)S(1)}, u32[]{:S(2)}, u32[]{:S(2)}) %collective-permute-start.15) | collective-permute-done | bytes 393248 | tf_op jit(solution)/shard_map/ppermute | solution.py:40
  89.9 0.1 slice_add_fusion.2
  90.0 1.6 %collective-permute-start.16 = (bf16[16,6144]{1,0:T(8,128)(2,1)S(1)}, bf16[16,6144]{1,0:T(8,128)(2,1)S(1)}, u32[]{:S(2)}, u32[]{:S(2)}) collective-permute-start(bf16[16,6144]{1,0:T(8,128)(2,1)S(1)} %slice.67), channel_id=1, source_target_pairs={{0,1},{1,0},{2,3},{3,2},{4,5},{5,4},{6,7},{7,6},{8,24},{9,25},{10,... | collective-permute-start | bytes 589832 | tf_op jit(solution)/shard_map/ppermute | solution.py:40
  91.6 4.7 %collective-permute-done.13 = bf16[32,6144]{1,0:T(8,128)(2,1)S(1)} collective-permute-done((bf16[32,6144]{1,0:T(8,128)(2,1)S(1)}, bf16[32,6144]{1,0:T(8,128)(2,1)S(1)}, u32[]{:S(2)}, u32[]{:S(2)}) %collective-permute-start.13) | collective-permute-done | bytes 393248 | tf_op jit(solution)/shard_map/ppermute | solution.py:40
  96.2 0.1 slice_add_fusion.3
  96.3 1.6 %collective-permute-start.14 = (bf16[16,6144]{1,0:T(8,128)(2,1)S(1)}, bf16[16,6144]{1,0:T(8,128)(2,1)S(1)}, u32[]{:S(2)}, u32[]{:S(2)}) collective-permute-start(bf16[16,6144]{1,0:T(8,128)(2,1)S(1)} %slice.65), channel_id=1, source_target_pairs={{0,1},{1,0},{2,3},{3,2},{4,5},{5,4},{6,7},{7,6},{8,24},{9,25},{10,... | collective-permute-start | bytes 589832 | tf_op jit(solution)/shard_map/ppermute | solution.py:40
  97.9 2.5 %collective-permute-start.23 = (bf16[16,6144]{1,0:T(8,128)(2,1)S(1)}, bf16[16,6144]{1,0:T(8,128)(2,1)S(1)}, u32[]{:S(2)}, u32[]{:S(2)}) collective-permute-start(bf16[16,6144]{1,0:T(8,128)(2,1)S(1)} %slice_add_fusion.4), channel_id=1, source_target_pairs={{0,6},{1,7},{2,4},{3,5},{4,2},{5,3},{6,0},{7,1},{8,14},{9,15},{10,... | collective-permute-start | bytes 589832 | tf_op jit(solution)/shard_map/ppermute | solution.py:40
  100.5 0.1 collective-permute-start.20
  100.6 1.9 %collective-permute-start.17 = (bf16[16,6144]{1,0:T(8,128)(2,1)S(1)}, bf16[16,6144]{1,0:T(8,128)(2,1)S(1)}, u32[]{:S(2)}, u32[]{:S(2)}) collective-permute-start(bf16[16,6144]{1,0:T(8,128)(2,1)S(1)} %slice_add_fusion.6), channel_id=1, source_target_pairs={{0,2},{1,3},{2,0},{3,1},{4,6},{5,7},{6,4},{7,5},{8,10},{9,11},{10,... | collective-permute-start | bytes 589832 | tf_op jit(solution)/shard_map/ppermute | solution.py:40
  102.6 4.5 %collective-permute-done.23 = bf16[16,6144]{1,0:T(8,128)(2,1)S(1)} collective-permute-done((bf16[16,6144]{1,0:T(8,128)(2,1)S(1)}, bf16[16,6144]{1,0:T(8,128)(2,1)S(1)}, u32[]{:S(2)}, u32[]{:S(2)}) %collective-permute-start.23) | collective-permute-done | bytes 196640 | tf_op jit(solution)/shard_map/ppermute | solution.py:40
  107.0 7.2 %collective-permute-done.20 = bf16[16,6144]{1,0:T(8,128)(2,1)S(1)} collective-permute-done((bf16[16,6144]{1,0:T(8,128)(2,1)S(1)}, bf16[16,6144]{1,0:T(8,128)(2,1)S(1)}, u32[]{:S(2)}, u32[]{:S(2)}) %collective-permute-start.20) | collective-permute-done | bytes 196640 | tf_op jit(solution)/shard_map/ppermute | solution.py:40
  114.2 0.8 add_convert_fusion
  (36 shorter events, 0.6 us)
Async XLA Ops:
  1.8 7.4 %collective-permute-start = (bf16[16,6272]{1,0:T(8,128)(2,1)}, bf16[16,6272]{1,0:T(8,128)(2,1)S(1)}, u32[]{:S(2)}, u32[]{:S(2)}) collective-permute-start(bf16[16,6272]{1,0:T(8,128)(2,1)} %prepare.1), channel_id=1, source_target_pairs={{0,1},{1,0},{2,3},{3,2},{4,5},{5,4},{6,7},{7,6},{8,24},{9,25},{10,... | collective-permute-start | bytes 602120 | tf_op jit(solution)/shard_map/ppermute | solution.py:40
  4.8 10.0 %collective-permute-start.8 = (bf16[16,6272]{1,0:T(8,128)(2,1)}, bf16[16,6272]{1,0:T(8,128)(2,1)S(1)}, u32[]{:S(2)}, u32[]{:S(2)}) collective-permute-start(bf16[16,6272]{1,0:T(8,128)(2,1)} %prepare.1), channel_id=1, source_target_pairs={{0,6},{1,7},{2,4},{3,5},{4,2},{5,3},{6,0},{7,1},{8,14},{9,15},{10,... | collective-permute-start | bytes 602120 | tf_op jit(solution)/shard_map/ppermute | solution.py:40
  8.4 17.0 %collective-permute-start.5 = (bf16[16,6272]{1,0:T(8,128)(2,1)}, bf16[16,6272]{1,0:T(8,128)(2,1)S(1)}, u32[]{:S(2)}, u32[]{:S(2)}) collective-permute-start(bf16[16,6272]{1,0:T(8,128)(2,1)} %prepare.1), channel_id=1, source_target_pairs={{0,4},{1,5},{2,6},{3,7},{4,0},{5,1},{6,2},{7,3},{8,12},{9,13},{10,... | collective-permute-start | bytes 602120 | tf_op jit(solution)/shard_map/ppermute | solution.py:40
  8.4 18.5 %collective-permute-start.2 = (bf16[16,6272]{1,0:T(8,128)(2,1)}, bf16[16,6272]{1,0:T(8,128)(2,1)S(1)}, u32[]{:S(2)}, u32[]{:S(2)}) collective-permute-start(bf16[16,6272]{1,0:T(8,128)(2,1)} %prepare.1), channel_id=1, source_target_pairs={{0,2},{1,3},{2,0},{3,1},{4,6},{5,7},{6,4},{7,5},{8,10},{9,11},{10,... | collective-permute-start | bytes 602120 | tf_op jit(solution)/shard_map/ppermute | solution.py:40
  9.2 41.5 %copy-start = (bf16[1,6144,1024]{2,1,0:T(8,128)(2,1)S(1)}, bf16[1,6144,1024]{2,1,0:T(8,128)(2,1)}, u32[]{:S(2)}) copy-start(bf16[1,6144,1024]{2,1,0:T(8,128)(2,1)} %gate.1) | copy-start | bytes 37748740
  10.3 27.9 %collective-permute-start.1 = (bf16[32,6272]{1,0:T(8,128)(2,1)S(1)}, bf16[32,6272]{1,0:T(8,128)(2,1)S(1)}, u32[]{:S(2)}, u32[]{:S(2)}) collective-permute-start(bf16[32,6272]{1,0:T(8,128)(2,1)S(1)} %pad_maximum_fusion.1), channel_id=1, source_target_pairs={{0,16},{1,17},{2,18},{3,19},{4,20},{5,21},{6,22},{7,23},{8,9},{9,8... | collective-permute-start | bytes 1204232 | tf_op jit(solution)/shard_map/ppermute | solution.py:40
  14.8 12.8 %collective-permute-start.9 = (bf16[16,6272]{1,0:T(8,128)(2,1)S(1)}, bf16[16,6272]{1,0:T(8,128)(2,1)S(1)}, u32[]{:S(2)}, u32[]{:S(2)}) collective-permute-start(bf16[16,6272]{1,0:T(8,128)(2,1)S(1)} %collective-permute-done.8), channel_id=1, source_target_pairs={{0,1},{1,0},{2,3},{3,2},{4,5},{5,4},{6,7},{7,6},{8,24},{9,25},{10,... | collective-permute-start | bytes 602120 | tf_op jit(solution)/shard_map/ppermute | solution.py:40
  25.4 7.7 %collective-permute-start.6 = (bf16[16,6272]{1,0:T(8,128)(2,1)S(1)}, bf16[16,6272]{1,0:T(8,128)(2,1)S(1)}, u32[]{:S(2)}, u32[]{:S(2)}) collective-permute-start(bf16[16,6272]{1,0:T(8,128)(2,1)S(1)} %collective-permute-done.5), channel_id=1, source_target_pairs={{0,1},{1,0},{2,3},{3,2},{4,5},{5,4},{6,7},{7,6},{8,24},{9,25},{10,... | collective-permute-start | bytes 602120 | tf_op jit(solution)/shard_map/ppermute | solution.py:40
  26.9 10.5 %collective-permute-start.3 = (bf16[16,6272]{1,0:T(8,128)(2,1)S(1)}, bf16[16,6272]{1,0:T(8,128)(2,1)S(1)}, u32[]{:S(2)}, u32[]{:S(2)}) collective-permute-start(bf16[16,6272]{1,0:T(8,128)(2,1)S(1)} %collective-permute-done.2), channel_id=1, source_target_pairs={{0,1},{1,0},{2,3},{3,2},{4,5},{5,4},{6,7},{7,6},{8,24},{9,25},{10,... | collective-permute-start | bytes 602120 | tf_op jit(solution)/shard_map/ppermute | solution.py:40
  27.6 11.7 %collective-permute-start.10 = (bf16[32,6272]{1,0:T(8,128)(2,1)S(1)}, bf16[32,6272]{1,0:T(8,128)(2,1)S(1)}, u32[]{:S(2)}, u32[]{:S(2)}) collective-permute-start(bf16[32,6272]{1,0:T(8,128)(2,1)S(1)} %pad_maximum_fusion.4), channel_id=1, source_target_pairs={{0,16},{1,17},{2,18},{3,19},{4,20},{5,21},{6,22},{7,23},{8,9},{9,8... | collective-permute-start | bytes 1204232 | tf_op jit(solution)/shard_map/ppermute | solution.py:40
  33.1 7.9 %collective-permute-start.7 = (bf16[32,6272]{1,0:T(8,128)(2,1)S(1)}, bf16[32,6272]{1,0:T(8,128)(2,1)S(1)}, u32[]{:S(2)}, u32[]{:S(2)}) collective-permute-start(bf16[32,6272]{1,0:T(8,128)(2,1)S(1)} %pad_maximum_fusion.3), channel_id=1, source_target_pairs={{0,16},{1,17},{2,18},{3,19},{4,20},{5,21},{6,22},{7,23},{8,9},{9,8... | collective-permute-start | bytes 1204232 | tf_op jit(solution)/shard_map/ppermute | solution.py:40
  37.5 7.9 %collective-permute-start.4 = (bf16[32,6272]{1,0:T(8,128)(2,1)S(1)}, bf16[32,6272]{1,0:T(8,128)(2,1)S(1)}, u32[]{:S(2)}, u32[]{:S(2)}) collective-permute-start(bf16[32,6272]{1,0:T(8,128)(2,1)S(1)} %pad_maximum_fusion.2), channel_id=1, source_target_pairs={{0,16},{1,17},{2,18},{3,19},{4,20},{5,21},{6,22},{7,23},{8,9},{9,8... | collective-permute-start | bytes 1204232 | tf_op jit(solution)/shard_map/ppermute | solution.py:40
  47.0 3.7 %collective-permute-start.11 = (bf16[128,6144]{1,0:T(8,128)(2,1)S(1)}, bf16[128,6144]{1,0:T(8,128)(2,1)S(1)}, u32[]{:S(2)}, u32[]{:S(2)}) collective-permute-start(bf16[128,6144]{1,0:T(8,128)(2,1)S(1)} %get-tuple-element.14), channel_id=1, source_target_pairs={{0,8},{1,9},{2,10},{3,11},{4,12},{5,13},{6,14},{7,15},{8,0},{9,1},... | collective-permute-start | bytes 4718600 | tf_op jit(solution)/shard_map/ppermute | solution.py:40
  63.5 3.5 %collective-permute-start.12 = (bf16[128,6144]{1,0:T(8,128)(2,1)S(1)}, bf16[128,6144]{1,0:T(8,128)(2,1)S(1)}, u32[]{:S(2)}, u32[]{:S(2)}) collective-permute-start(bf16[128,6144]{1,0:T(8,128)(2,1)S(1)} %get-tuple-element.16), channel_id=1, source_target_pairs={{0,8},{1,9},{2,10},{3,11},{4,12},{5,13},{6,14},{7,15},{8,0},{9,1},... | collective-permute-start | bytes 4718600 | tf_op jit(solution)/shard_map/ppermute | solution.py:40
  69.4 7.8 %collective-permute-start.21 = (bf16[32,6144]{1,0:T(8,128)(2,1)S(1)}, bf16[32,6144]{1,0:T(8,128)(2,1)S(1)}, u32[]{:S(2)}, u32[]{:S(2)}) collective-permute-start(bf16[32,6144]{1,0:T(8,128)(2,1)S(1)} %slice.61), channel_id=1, source_target_pairs={{0,16},{1,17},{2,18},{3,19},{4,20},{5,21},{6,22},{7,23},{8,9},{9,8... | collective-permute-start | bytes 1179656 | tf_op jit(solution)/shard_map/ppermute | solution.py:40
  70.1 13.4 %collective-permute-start.18 = (bf16[32,6144]{1,0:T(8,128)(2,1)S(1)}, bf16[32,6144]{1,0:T(8,128)(2,1)S(1)}, u32[]{:S(2)}, u32[]{:S(2)}) collective-permute-start(bf16[32,6144]{1,0:T(8,128)(2,1)S(1)} %slice.57), channel_id=1, source_target_pairs={{0,16},{1,17},{2,18},{3,19},{4,20},{5,21},{6,22},{7,23},{8,9},{9,8... | collective-permute-start | bytes 1179656 | tf_op jit(solution)/shard_map/ppermute | solution.py:40
  71.7 18.2 %collective-permute-start.15 = (bf16[32,6144]{1,0:T(8,128)(2,1)S(1)}, bf16[32,6144]{1,0:T(8,128)(2,1)S(1)}, u32[]{:S(2)}, u32[]{:S(2)}) collective-permute-start(bf16[32,6144]{1,0:T(8,128)(2,1)S(1)} %slice.53), channel_id=1, source_target_pairs={{0,16},{1,17},{2,18},{3,19},{4,20},{5,21},{6,22},{7,23},{8,9},{9,8... | collective-permute-start | bytes 1179656 | tf_op jit(solution)/shard_map/ppermute | solution.py:40
  72.2 24.1 %collective-permute-start.13 = (bf16[32,6144]{1,0:T(8,128)(2,1)S(1)}, bf16[32,6144]{1,0:T(8,128)(2,1)S(1)}, u32[]{:S(2)}, u32[]{:S(2)}) collective-permute-start(bf16[32,6144]{1,0:T(8,128)(2,1)S(1)} %slice.49), channel_id=1, source_target_pairs={{0,16},{1,17},{2,18},{3,19},{4,20},{5,21},{6,22},{7,23},{8,9},{9,8... | collective-permute-start | bytes 1179656 | tf_op jit(solution)/shard_map/ppermute | solution.py:40
  77.4 20.5 %collective-permute-start.22 = (bf16[16,6144]{1,0:T(8,128)(2,1)S(1)}, bf16[16,6144]{1,0:T(8,128)(2,1)S(1)}, u32[]{:S(2)}, u32[]{:S(2)}) collective-permute-start(bf16[16,6144]{1,0:T(8,128)(2,1)S(1)} %slice.71), channel_id=1, source_target_pairs={{0,1},{1,0},{2,3},{3,2},{4,5},{5,4},{6,7},{7,6},{8,24},{9,25},{10,... | collective-permute-start | bytes 589832 | tf_op jit(solution)/shard_map/ppermute | solution.py:40
  83.5 16.9 %collective-permute-start.19 = (bf16[16,6144]{1,0:T(8,128)(2,1)S(1)}, bf16[16,6144]{1,0:T(8,128)(2,1)S(1)}, u32[]{:S(2)}, u32[]{:S(2)}) collective-permute-start(bf16[16,6144]{1,0:T(8,128)(2,1)S(1)} %slice.69), channel_id=1, source_target_pairs={{0,1},{1,0},{2,3},{3,2},{4,5},{5,4},{6,7},{7,6},{8,24},{9,25},{10,... | collective-permute-start | bytes 589832 | tf_op jit(solution)/shard_map/ppermute | solution.py:40
  90.0 10.6 %collective-permute-start.16 = (bf16[16,6144]{1,0:T(8,128)(2,1)S(1)}, bf16[16,6144]{1,0:T(8,128)(2,1)S(1)}, u32[]{:S(2)}, u32[]{:S(2)}) collective-permute-start(bf16[16,6144]{1,0:T(8,128)(2,1)S(1)} %slice.67), channel_id=1, source_target_pairs={{0,1},{1,0},{2,3},{3,2},{4,5},{5,4},{6,7},{7,6},{8,24},{9,25},{10,... | collective-permute-start | bytes 589832 | tf_op jit(solution)/shard_map/ppermute | solution.py:40
  96.3 6.2 %collective-permute-start.14 = (bf16[16,6144]{1,0:T(8,128)(2,1)S(1)}, bf16[16,6144]{1,0:T(8,128)(2,1)S(1)}, u32[]{:S(2)}, u32[]{:S(2)}) collective-permute-start(bf16[16,6144]{1,0:T(8,128)(2,1)S(1)} %slice.65), channel_id=1, source_target_pairs={{0,1},{1,0},{2,3},{3,2},{4,5},{5,4},{6,7},{7,6},{8,24},{9,25},{10,... | collective-permute-start | bytes 589832 | tf_op jit(solution)/shard_map/ppermute | solution.py:40
  97.9 9.1 %collective-permute-start.23 = (bf16[16,6144]{1,0:T(8,128)(2,1)S(1)}, bf16[16,6144]{1,0:T(8,128)(2,1)S(1)}, u32[]{:S(2)}, u32[]{:S(2)}) collective-permute-start(bf16[16,6144]{1,0:T(8,128)(2,1)S(1)} %slice_add_fusion.4), channel_id=1, source_target_pairs={{0,6},{1,7},{2,4},{3,5},{4,2},{5,3},{6,0},{7,1},{8,14},{9,15},{10,... | collective-permute-start | bytes 589832 | tf_op jit(solution)/shard_map/ppermute | solution.py:40
  100.5 13.7 %collective-permute-start.20 = (bf16[16,6144]{1,0:T(8,128)(2,1)S(1)}, bf16[16,6144]{1,0:T(8,128)(2,1)S(1)}, u32[]{:S(2)}, u32[]{:S(2)}) collective-permute-start(bf16[16,6144]{1,0:T(8,128)(2,1)S(1)} %slice_add_fusion.5), channel_id=1, source_target_pairs={{0,4},{1,5},{2,6},{3,7},{4,0},{5,1},{6,2},{7,3},{8,12},{9,13},{10,... | collective-permute-start | bytes 589832 | tf_op jit(solution)/shard_map/ppermute | solution.py:40
  100.6 13.6 %collective-permute-start.17 = (bf16[16,6144]{1,0:T(8,128)(2,1)S(1)}, bf16[16,6144]{1,0:T(8,128)(2,1)S(1)}, u32[]{:S(2)}, u32[]{:S(2)}) collective-permute-start(bf16[16,6144]{1,0:T(8,128)(2,1)S(1)} %slice_add_fusion.6), channel_id=1, source_target_pairs={{0,2},{1,3},{2,0},{3,1},{4,6},{5,7},{6,4},{7,5},{8,10},{9,11},{10,... | collective-permute-start | bytes 589832 | tf_op jit(solution)/shard_map/ppermute | solution.py:40

commit v2 on v1

--- a/solution.py
+++ b/solution.py
@@ -10,10 +10,10 @@
 
 CAP = 8
 META = 128
-FFT = 256
-OUT = 1024
-PLACE = 2048
-MIX = 2048
+FFT = 512
+OUT = 2048
+PLACE = 3072
+MIX = 3072
 FFN_VMEM = 32 * 2**20
 AXES = ("expert", "mp")
 
@@ -59,18 +59,25 @@
 
 
 def gather_z(grid, own):
-    blocks = [own] + [None] * (grid.z - 1)
-    for k in reversed(range(1, grid.z)):
-        blocks[k] = grid.move(own, grid.across_z(k))
-    return blocks
+    if grid.z != 4:
+        return [own] + [grid.move(own, grid.across_z(k)) for k in range(1, grid.z)]
+    far = grid.move(own, grid.across_z(2))
+    near = grid.move(own, grid.across_z(1))
+    last = grid.move(far, grid.across_z(1))
+    return [own, near, far, last]
 
 
 def scatter_z(grid, parts):
-    total = parts[0].astype(jnp.float32)
-    for k in range(1, grid.z):
-        moved = grid.move(parts[k], grid.across_z(k, -1))
-        total = total + moved.astype(jnp.float32)
-    return total.astype(jnp.bfloat16)
+    f32 = jnp.float32
+    if grid.z != 4:
+        moved = [grid.move(parts[k], grid.across_z(k, -1)) for k in range(1, grid.z)]
+        return sum([m.astype(f32) for m in moved], parts[0].astype(f32)).astype(jnp.bfloat16)
+    own, near, far, last = parts
+    last = grid.move(last, grid.across_z(1))
+    far = far + last
+    far = grid.move(far, grid.across_z(2))
+    near = grid.move(near, grid.across_z(1))
+    return (own.astype(f32) + far.astype(f32) + near.astype(f32)).astype(jnp.bfloat16)
 
 
 def spread(grid, block):
@@ -175,14 +182,17 @@
     )(*groups)
 
 
-def ffn_kernel(features, mine, theirs, gate, up_hbm, down_hbm, out_mine, out_theirs, *scratch):
+def ffn_kernel(features, n, *refs):
     f32, bf16 = jnp.float32, jnp.bfloat16
-    up, down, gated, hidden, up_sems, down_sems = scratch
-    width, each = gate.shape[2], mine.shape[0]
+    blocks, refs = refs[:n], refs[n:]
+    gate, up_hbm, down_hbm = refs[:3]
+    outs, refs = refs[3:7], refs[7:]
+    up, down, gated, hidden, up_sems, down_sems = refs
+    width, some = gate.shape[2], outs[0].shape[0]
     up_tiles, down_tiles = width // FFT, features // OUT
 
     def piece():
-        return jnp.concatenate([mine[...], theirs[...]], axis=0)
+        return jnp.concatenate([block[...] for block in blocks], axis=0)
 
     def tile(i, size):
         return pl.ds(pl.multiple_of(i * size, size), size)
@@ -218,28 +228,28 @@
         place = tile(i, OUT)
         product = jnp.dot(hidden[...], down[:, place], preferred_element_type=f32)
         product = product.astype(bf16)
-        out_mine[:, place] = product[:each]
-        out_theirs[:, place] = product[each:]
+        for at, out in enumerate(outs):
+            out[:, place] = product[at * some : (at + 1) * some]
 
 
 def ffn(mine, theirs, w_gate, w_up, w_down):
     bf16 = jnp.bfloat16
-    each, features = mine.shape
+    each, features = sum(m.shape[0] for m in mine), mine[0].shape[1]
     width = w_gate.shape[2]
     need = 2 * (3 * features * width + 4 * each * features + 2 * each * width)
     if need > 56 * 2**20 or width % FFT or features % OUT:
-        piece = jnp.concatenate([mine, theirs], axis=0)
+        piece = jnp.concatenate(mine + theirs, axis=0)
         gate_proj = jnp.dot(piece, w_gate[0], preferred_element_type=jnp.float32)
         up_proj = jnp.dot(piece, w_up[0], preferred_element_type=jnp.float32)
         hidden = (jax.nn.silu(gate_proj) * up_proj).astype(bf16)
         product = jnp.dot(hidden, w_down[0], preferred_element_type=jnp.float32).astype(bf16)
-        return product[:each], product[each:]
+        return [product[at * each // 2 : (at + 1) * each // 2] for at in range(4)]
     vmem, hbm = pl.BlockSpec(memory_space=pltpu.VMEM), pl.BlockSpec(memory_space=pltpu.HBM)
     return pl.pallas_call(
-        functools.partial(ffn_kernel, features),
-        out_shape=[jax.ShapeDtypeStruct(mine.shape, bf16)] * 2,
-        in_specs=[vmem] * 3 + [hbm] * 2,
-        out_specs=[vmem] * 2,
+        functools.partial(ffn_kernel, features, len(mine + theirs)),
+        out_shape=[jax.ShapeDtypeStruct((each // 2, features), bf16)] * 4,
+        in_specs=[vmem] * (len(mine + theirs) + 1) + [hbm] * 2,
+        out_specs=[vmem] * 4,
         scratch_shapes=[
             pltpu.VMEM((features, width), bf16),
             pltpu.VMEM((width, features), bf16),
@@ -255,7 +265,7 @@
         ),
         compiler_params=pltpu.CompilerParams(vmem_limit_bytes=FFN_VMEM),
         name="ffn",
-    )(mine, theirs, w_gate, w_up, w_down)
+    )(*mine, *theirs, w_gate, w_up, w_down)
 
 
 def mix_kernel(n, tok_rows, features, *refs):
@@ -308,13 +318,22 @@
     tok_rows, features = tokens.shape
     own = prepare(tokens, norm_gain, expert_ids, slot_ids, route_weights)
     groups = [spread(grid, block) for block in gather_z(grid, own)]
-    mine, away = place_rows(groups, tok_rows, features)
-    theirs = grid.move(away, grid.sibling)
-    mine, away = ffn(mine, theirs, w_gate, w_up, w_down)
-    theirs = grid.move(away, grid.sibling)
-    parts = list(mix(groups, mine, theirs, tok_rows))
-    for k in reversed(range(grid.z)):
-        parts[k] = fold(grid, parts[k])
+    mine, theirs = [], []
+    for some in (groups[:-1], groups[-1:]):
+        kept, away = place_rows(some, tok_rows, features)
+        mine.append(kept)
+        theirs.append(grid.move(away, grid.sibling))
+    results = ffn(mine, theirs, w_gate, w_up, w_down)
+    moved = [None, None]
+    for side in (1, 0):
+        moved[side] = grid.move(results[2 + side], grid.sibling)
+    parts = [None] * grid.z
+    some = grid.z // 2
+    for side in (1, 0):
+        held = groups[side * some : (side + 1) * some]
+        mixed = mix(held, results[side], moved[side], tok_rows)
+        for k in reversed(range(some)):
+            parts[side * some + k] = fold(grid, mixed[k])
     return scatter_z(grid, parts)
 
 

time: 115 us -> 106 us (0.922)
  waiting for transfers between devices: 62.9 us -> 52.3 us
  starting transfers between devices: 29.6 us -> 32.4 us
  Pallas kernels: 18.6 us -> 17.4 us
    ppermute x24 -> x26, waiting for transfers between devices: 62.9 us -> 52.3 us  [move(): return lax.ppermute(value, AXES, pairs)]
    ppermute x24 -> x26, starting transfers between devices: 29.6 us -> 32.4 us  [move(): return lax.ppermute(value, AXES, pairs)]
    pallas_call x1, Pallas kernels: 12.8 us -> 11.2 us  [ffn(): pl.pallas_call(functools.partial(ffn_kernel, features, len(mine + theirs)...]
    pallas_call x1 -> x2, Pallas kernels: 2.38 us -> 2.54 us  [mix(): pl.pallas_call(functools.partial(mix_kernel, n, tok_rows, features), grid...]
  transfers between devices with their start and end apart: 24 -> 26, of which waited for: 14 -> 15; matrix products, arithmetic and copies ran while one was open for 2% -> 3% of each run, Pallas kernels for 0% -> 4%
where the time goes in v2:
time: 106 us
  waiting for transfers between devices  52.3 us (49%)
  starting transfers between devices  32.4 us (31%)
  Pallas kernels  17.4 us (16%)
  other arithmetic  3.19 us (3%)
    ppermute x26, waiting for transfers between devices, move(): return lax.ppermute(value, AXES, pairs)  52.3 us
    ppermute x26, starting transfers between devices, move(): return lax.ppermute(value, AXES, pairs)  32.4 us
    pallas_call x1, Pallas kernels, ffn(): pl.pallas_call(functools.partial(ffn_kernel, features, len(mine + theirs)...  11.2 us
    pallas_call x2, Pallas kernels, mix(): pl.pallas_call(functools.partial(mix_kernel, n, tok_rows, features), grid...  2.54 us
  transfers between devices with their start and end apart: 26, of which 15 were waited for; matrix products, arithmetic and copies ran while one was open for 3% of the time, Pallas kernels for 4%

profile of v2, /device:TPU:0, one launch (start us, length us, event | category | flops | bytes accessed | tf_op | source)
XLA Modules:
  0.0 106.0 jit_solution(7904327558298756050)
XLA Ops:
  0.0 1.8 %prepare.1 = bf16[16,6272]{1,0:T(8,128)(2,1)} custom-call(bf16[16,6144]{1,0:T(8,128)(2,1)} %tok_ref.1, bf16[48,128]{1,0:T(8,128)(2,1)} %bitcast.4, s32[2,16]{1,0:T(2,128)} %bitcast.5, s32[2,16]{1,0:T(2,128)} %bitcast.6, f32[2,16]{1,0:T(2,128)} %bitcast.7), custom_call_target="tpu_custom_call" | custom-call | tf_op jit(solution)/shard_map/prepare/pallas_call | solution.py:127
  1.8 3.0 %collective-permute-start = (bf16[16,6272]{1,0:T(8,128)(2,1)}, bf16[16,6272]{1,0:T(8,128)(2,1)S(1)}, u32[]{:S(2)}, u32[]{:S(2)}) collective-permute-start(bf16[16,6272]{1,0:T(8,128)(2,1)} %prepare.1), channel_id=1, source_target_pairs={{0,1},{1,0},{2,3},{3,2},{4,5},{5,4},{6,7},{7,6},{8,24},{9,25},{10,... | collective-permute-start | bytes 602120 | tf_op jit(solution)/shard_map/ppermute | solution.py:40
  4.8 2.6 %collective-permute-start.5 = (bf16[16,6272]{1,0:T(8,128)(2,1)}, bf16[16,6272]{1,0:T(8,128)(2,1)S(1)}, u32[]{:S(2)}, u32[]{:S(2)}) collective-permute-start(bf16[16,6272]{1,0:T(8,128)(2,1)} %prepare.1), channel_id=1, source_target_pairs={{0,4},{1,5},{2,6},{3,7},{4,0},{5,1},{6,2},{7,3},{8,12},{9,13},{10,... | collective-permute-start | bytes 602120 | tf_op jit(solution)/shard_map/ppermute | solution.py:40
  7.4 1.6 %collective-permute-start.2 = (bf16[16,6272]{1,0:T(8,128)(2,1)}, bf16[16,6272]{1,0:T(8,128)(2,1)S(1)}, u32[]{:S(2)}, u32[]{:S(2)}) collective-permute-start(bf16[16,6272]{1,0:T(8,128)(2,1)} %prepare.1), channel_id=1, source_target_pairs={{0,2},{1,3},{2,0},{3,1},{4,6},{5,7},{6,4},{7,5},{8,10},{9,11},{10,... | collective-permute-start | bytes 602120 | tf_op jit(solution)/shard_map/ppermute | solution.py:40
  9.0 1.1 %pad_maximum_fusion.1 = bf16[32,6272]{1,0:T(8,128)(2,1)S(1)} fusion(bf16[16,6272]{1,0:T(8,128)(2,1)S(1)} %collective-permute-done, bf16[16,6272]{1,0:T(8,128)(2,1)} %prepare.1), kind=kLoop, calls=%fused_computation.1 | loop fusion | flops 802816 | bytes 802816 | tf_op jit(solution)/shard_map/concatenate | solution.py:85
  10.1 1.8 %collective-permute-start.1 = (bf16[32,6272]{1,0:T(8,128)(2,1)S(1)}, bf16[32,6272]{1,0:T(8,128)(2,1)S(1)}, u32[]{:S(2)}, u32[]{:S(2)}) collective-permute-start(bf16[32,6272]{1,0:T(8,128)(2,1)S(1)} %pad_maximum_fusion.1), channel_id=1, source_target_pairs={{0,16},{1,17},{2,18},{3,19},{4,20},{5,21},{6,22},{7,23},{8,9},{9,8... | collective-permute-start | bytes 1204232 | tf_op jit(solution)/shard_map/ppermute | solution.py:40
  11.9 4.9 %collective-permute-done.5 = bf16[16,6272]{1,0:T(8,128)(2,1)S(1)} collective-permute-done((bf16[16,6272]{1,0:T(8,128)(2,1)}, bf16[16,6272]{1,0:T(8,128)(2,1)S(1)}, u32[]{:S(2)}, u32[]{:S(2)}) %collective-permute-start.5) | collective-permute-done | bytes 200736 | tf_op jit(solution)/shard_map/ppermute | solution.py:40
  16.8 0.7 collective-permute-start.8
  17.5 1.5 %collective-permute-start.6 = (bf16[16,6272]{1,0:T(8,128)(2,1)S(1)}, bf16[16,6272]{1,0:T(8,128)(2,1)S(1)}, u32[]{:S(2)}, u32[]{:S(2)}) collective-permute-start(bf16[16,6272]{1,0:T(8,128)(2,1)S(1)} %collective-permute-done.5), channel_id=1, source_target_pairs={{0,1},{1,0},{2,3},{3,2},{4,5},{5,4},{6,7},{7,6},{8,24},{9,25},{10,... | collective-permute-start | bytes 602120 | tf_op jit(solution)/shard_map/ppermute | solution.py:40
  19.0 0.6 collective-permute-start.3
  19.6 3.6 %collective-permute-done.6 = bf16[16,6272]{1,0:T(8,128)(2,1)S(1)} collective-permute-done((bf16[16,6272]{1,0:T(8,128)(2,1)S(1)}, bf16[16,6272]{1,0:T(8,128)(2,1)S(1)}, u32[]{:S(2)}, u32[]{:S(2)}) %collective-permute-start.6) | collective-permute-done | bytes 200736 | tf_op jit(solution)/shard_map/ppermute | solution.py:40
  23.2 0.6 collective-permute-start.7
  23.8 2.1 %collective-permute-done.3 = bf16[16,6272]{1,0:T(8,128)(2,1)S(1)} collective-permute-done((bf16[16,6272]{1,0:T(8,128)(2,1)S(1)}, bf16[16,6272]{1,0:T(8,128)(2,1)S(1)}, u32[]{:S(2)}, u32[]{:S(2)}) %collective-permute-start.3) | collective-permute-done | bytes 200736 | tf_op jit(solution)/shard_map/ppermute | solution.py:40
  25.9 0.8 collective-permute-start.4
  26.7 1.3 %collective-permute-start.9 = (bf16[16,6272]{1,0:T(8,128)(2,1)S(1)}, bf16[16,6272]{1,0:T(8,128)(2,1)S(1)}, u32[]{:S(2)}, u32[]{:S(2)}) collective-permute-start(bf16[16,6272]{1,0:T(8,128)(2,1)S(1)} %collective-permute-done.8), channel_id=1, source_target_pairs={{0,1},{1,0},{2,3},{3,2},{4,5},{5,4},{6,7},{7,6},{8,24},{9,25},{10,... | collective-permute-start | bytes 602120 | tf_op jit(solution)/shard_map/ppermute | solution.py:40
  28.1 6.5 %collective-permute-done.9 = bf16[16,6272]{1,0:T(8,128)(2,1)S(1)} collective-permute-done((bf16[16,6272]{1,0:T(8,128)(2,1)S(1)}, bf16[16,6272]{1,0:T(8,128)(2,1)S(1)}, u32[]{:S(2)}, u32[]{:S(2)}) %collective-permute-start.9) | collective-permute-done | bytes 200736 | tf_op jit(solution)/shard_map/ppermute | solution.py:40
  34.6 1.4 %collective-permute-start.10 = (bf16[32,6272]{1,0:T(8,128)(2,1)S(1)}, bf16[32,6272]{1,0:T(8,128)(2,1)S(1)}, u32[]{:S(2)}, u32[]{:S(2)}) collective-permute-start(bf16[32,6272]{1,0:T(8,128)(2,1)S(1)} %pad_maximum_fusion.4), channel_id=1, source_target_pairs={{0,16},{1,17},{2,18},{3,19},{4,20},{5,21},{6,22},{7,23},{8,9},{9,8... | collective-permute-start | bytes 1204232 | tf_op jit(solution)/shard_map/ppermute | solution.py:40
  36.0 1.0 pad_maximum_fusion.refs_0_
  37.1 0.5 collective-permute-done.4
  37.6 1.2 %place.2 = (bf16[96,6144]{1,0:T(8,128)(2,1)S(1)}, bf16[96,6144]{1,0:T(8,128)(2,1)S(1)}) custom-call(bf16[64,6272]{1,0:T(8,128)(2,1)S(1)} %pad_maximum_fusion.refs_0_, bf16[64,6272]{1,0:T(8,128)(2,1)S(1)} %constant_dynamic-update-slice_fusion.refs_1_, bf16[64,6272]{1,0:T(8,128)(2,1)S(1)} %constant_dynamic-update-slice_fusion.3.refs_2_.refs_0_), custom_call_target="tpu_custom_call" | custom-call | flops 452984832 | bytes 4718592 | tf_op jit(solution)/shard_map/place/pallas_call | solution.py:172
  38.9 3.6 %collective-permute-done.10 = bf16[32,6272]{1,0:T(8,128)(2,1)S(1)} collective-permute-done((bf16[32,6272]{1,0:T(8,128)(2,1)S(1)}, bf16[32,6272]{1,0:T(8,128)(2,1)S(1)}, u32[]{:S(2)}, u32[]{:S(2)}) %collective-permute-start.10) | collective-permute-done | bytes 401440 | tf_op jit(solution)/shard_map/ppermute | solution.py:40
  42.6 0.7 place.3
  43.3 1.7 %collective-permute-done.12.refs_3_ = bf16[32,6144]{1,0:T(8,128)(2,1)S(1)} collective-permute-done((bf16[32,6144]{1,0:T(8,128)(2,1)S(1)}, bf16[32,6144]{1,0:T(8,128)(2,1)S(1)}, u32[]{:S(2)}, u32[]{:S(2)}) %collective-permute-start.12) | collective-permute-done | bytes 393248 | tf_op jit(solution)/shard_map/ppermute | solution.py:40
  45.0 11.2 %ffn.1 = (bf16[64,6144]{1,0:T(8,128)(2,1)S(1)}, bf16[64,6144]{1,0:T(8,128)(2,1)S(1)}, bf16[64,6144]{1,0:T(8,128)(2,1)S(1)}, bf16[64,6144]{1,0:T(8,128)(2,1)S(1)}) custom-call(bf16[96,6144]{1,0:T(8,128)(2,1)S(1)} %get-tuple-element.17.refs_0_, bf16[32,6144]{1,0:T(8,128)(2,1)S(1)} %get-tuple-element.18.refs_1_, ...), custom_call_target="tpu_custom_call" | custom-call | flops 9663676416 | bytes 37748736 | tf_op jit(solution)/shard_map/ffn/pallas_call | solution.py:248
  56.2 0.2 collective-permute-start.13
  56.4 0.4 collective-permute-start.16
  56.8 1.8 %collective-permute-done.13.refs_3_ = bf16[64,6144]{1,0:T(8,128)(2,1)S(1)} collective-permute-done((bf16[64,6144]{1,0:T(8,128)(2,1)S(1)}, bf16[64,6144]{1,0:T(8,128)(2,1)S(1)}, u32[]{:S(2)}, u32[]{:S(2)}) %collective-permute-start.13) | collective-permute-done | bytes 786464 | tf_op jit(solution)/shard_map/ppermute | solution.py:40
  58.6 1.3 %mix.2 = (bf16[64,6144]{1,0:T(8,128)(2,1)S(1)}, bf16[64,6144]{1,0:T(8,128)(2,1)S(1)}) custom-call(bf16[64,6272]{1,0:T(8,128)(2,1)S(1)} %pad_maximum_fusion.refs_0_, bf16[64,6272]{1,0:T(8,128)(2,1)S(1)} %constant_dynamic-update-slice_fusion.refs_1_, bf16[64,6144]{1,0:T(8,128)(2,1)S(1)} %get-tuple-element.21.refs_2_, ...), custom_call_target="tpu_custom_call" | custom-call | flops 402653184 | bytes 3145728 | tf_op jit(solution)/shard_map/mix/pallas_call | solution.py:301
  59.9 1.4 %collective-permute-start.23 = (bf16[32,6144]{1,0:T(8,128)(2,1)S(1)}, bf16[32,6144]{1,0:T(8,128)(2,1)S(1)}, u32[]{:S(2)}, u32[]{:S(2)}) collective-permute-start(bf16[32,6144]{1,0:T(8,128)(2,1)S(1)} %slice.61), channel_id=1, source_target_pairs={{0,16},{1,17},{2,18},{3,19},{4,20},{5,21},{6,22},{7,23},{8,9},{9,8... | collective-permute-start | bytes 1179656 | tf_op jit(solution)/shard_map/ppermute | solution.py:40
  61.3 0.8 collective-permute-start.14
  62.1 1.3 %mix.3 = (bf16[64,6144]{1,0:T(8,128)(2,1)S(1)}, bf16[64,6144]{1,0:T(8,128)(2,1)S(1)}) custom-call(bf16[64,6272]{1,0:T(8,128)(2,1)S(1)} %constant_dynamic-update-slice_fusion.3.refs_2_.refs_0_, bf16[64,6272]{1,0:T(8,128)(2,1)S(1)} %constant_dynamic-update-slice_fusion.6.refs_0_.refs_1_, bf16[64,6144]{1,0:T(8,128)(2,1)S(1)} %get-tuple-element.24.refs_2_, ...), custom_call_target="tpu_custom_call" | custom-call | flops 402653184 | bytes 3145728 | tf_op jit(solution)/shard_map/mix/pallas_call | solution.py:301
  63.4 1.4 %collective-permute-start.19 = (bf16[32,6144]{1,0:T(8,128)(2,1)S(1)}, bf16[32,6144]{1,0:T(8,128)(2,1)S(1)}, u32[]{:S(2)}, u32[]{:S(2)}) collective-permute-start(bf16[32,6144]{1,0:T(8,128)(2,1)S(1)} %slice.57), channel_id=1, source_target_pairs={{0,16},{1,17},{2,18},{3,19},{4,20},{5,21},{6,22},{7,23},{8,9},{9,8... | collective-permute-start | bytes 1179656 | tf_op jit(solution)/shard_map/ppermute | solution.py:40
  64.8 0.7 collective-permute-start.17
  65.5 2.2 %collective-permute-done.23 = bf16[32,6144]{1,0:T(8,128)(2,1)S(1)} collective-permute-done((bf16[32,6144]{1,0:T(8,128)(2,1)S(1)}, bf16[32,6144]{1,0:T(8,128)(2,1)S(1)}, u32[]{:S(2)}, u32[]{:S(2)}) %collective-permute-start.23) | collective-permute-done | bytes 393248 | tf_op jit(solution)/shard_map/ppermute | solution.py:40
  67.8 1.3 %collective-permute-start.24 = (bf16[16,6144]{1,0:T(8,128)(2,1)S(1)}, bf16[16,6144]{1,0:T(8,128)(2,1)S(1)}, u32[]{:S(2)}, u32[]{:S(2)}) collective-permute-start(bf16[16,6144]{1,0:T(8,128)(2,1)S(1)} %slice.71), channel_id=1, source_target_pairs={{0,1},{1,0},{2,3},{3,2},{4,5},{5,4},{6,7},{7,6},{8,24},{9,25},{10,... | collective-permute-start | bytes 589832 | tf_op jit(solution)/shard_map/ppermute | solution.py:40
  69.1 5.0 %collective-permute-done.14 = bf16[32,6144]{1,0:T(8,128)(2,1)S(1)} collective-permute-done((bf16[32,6144]{1,0:T(8,128)(2,1)S(1)}, bf16[32,6144]{1,0:T(8,128)(2,1)S(1)}, u32[]{:S(2)}, u32[]{:S(2)}) %collective-permute-start.14) | collective-permute-done | bytes 393248 | tf_op jit(solution)/shard_map/ppermute | solution.py:40
  74.2 1.3 %collective-permute-start.15 = (bf16[16,6144]{1,0:T(8,128)(2,1)S(1)}, bf16[16,6144]{1,0:T(8,128)(2,1)S(1)}, u32[]{:S(2)}, u32[]{:S(2)}) collective-permute-start(bf16[16,6144]{1,0:T(8,128)(2,1)S(1)} %slice.65), channel_id=1, source_target_pairs={{0,1},{1,0},{2,3},{3,2},{4,5},{5,4},{6,7},{7,6},{8,24},{9,25},{10,... | collective-permute-start | bytes 589832 | tf_op jit(solution)/shard_map/ppermute | solution.py:40
  75.5 4.9 %collective-permute-done.19 = bf16[32,6144]{1,0:T(8,128)(2,1)S(1)} collective-permute-done((bf16[32,6144]{1,0:T(8,128)(2,1)S(1)}, bf16[32,6144]{1,0:T(8,128)(2,1)S(1)}, u32[]{:S(2)}, u32[]{:S(2)}) %collective-permute-start.19) | collective-permute-done | bytes 393248 | tf_op jit(solution)/shard_map/ppermute | solution.py:40
  80.6 1.3 %collective-permute-start.20 = (bf16[16,6144]{1,0:T(8,128)(2,1)S(1)}, bf16[16,6144]{1,0:T(8,128)(2,1)S(1)}, u32[]{:S(2)}, u32[]{:S(2)}) collective-permute-start(bf16[16,6144]{1,0:T(8,128)(2,1)S(1)} %slice.69), channel_id=1, source_target_pairs={{0,1},{1,0},{2,3},{3,2},{4,5},{5,4},{6,7},{7,6},{8,24},{9,25},{10,... | collective-permute-start | bytes 589832 | tf_op jit(solution)/shard_map/ppermute | solution.py:40
  81.9 4.9 %collective-permute-done.17 = bf16[32,6144]{1,0:T(8,128)(2,1)S(1)} collective-permute-done((bf16[32,6144]{1,0:T(8,128)(2,1)S(1)}, bf16[32,6144]{1,0:T(8,128)(2,1)S(1)}, u32[]{:S(2)}, u32[]{:S(2)}) %collective-permute-start.17) | collective-permute-done | bytes 393248 | tf_op jit(solution)/shard_map/ppermute | solution.py:40
  86.9 1.3 %collective-permute-start.18 = (bf16[16,6144]{1,0:T(8,128)(2,1)S(1)}, bf16[16,6144]{1,0:T(8,128)(2,1)S(1)}, u32[]{:S(2)}, u32[]{:S(2)}) collective-permute-start(bf16[16,6144]{1,0:T(8,128)(2,1)S(1)} %slice.67), channel_id=1, source_target_pairs={{0,1},{1,0},{2,3},{3,2},{4,5},{5,4},{6,7},{7,6},{8,24},{9,25},{10,... | collective-permute-start | bytes 589832 | tf_op jit(solution)/shard_map/ppermute | solution.py:40
  88.2 1.8 %collective-permute-start.21 = (bf16[16,6144]{1,0:T(8,128)(2,1)S(1)}, bf16[16,6144]{1,0:T(8,128)(2,1)S(1)}, u32[]{:S(2)}, u32[]{:S(2)}) collective-permute-start(bf16[16,6144]{1,0:T(8,128)(2,1)S(1)} %slice_add_fusion.5), channel_id=1, source_target_pairs={{0,2},{1,3},{2,0},{3,1},{4,6},{5,7},{6,4},{7,5},{8,10},{9,11},{10,... | collective-permute-start | bytes 589832 | tf_op jit(solution)/shard_map/ppermute | solution.py:40
  90.0 0.4 collective-permute-start.25
  90.4 2.2 %collective-permute-done.18 = bf16[16,6144]{1,0:T(8,128)(2,1)S(1)} collective-permute-done((bf16[16,6144]{1,0:T(8,128)(2,1)S(1)}, bf16[16,6144]{1,0:T(8,128)(2,1)S(1)}, u32[]{:S(2)}, u32[]{:S(2)}) %collective-permute-start.18) | collective-permute-done | bytes 196640 | tf_op jit(solution)/shard_map/ppermute | solution.py:40
  92.6 2.5 %collective-permute-done.21 = bf16[16,6144]{1,0:T(8,128)(2,1)S(1)} collective-permute-done((bf16[16,6144]{1,0:T(8,128)(2,1)S(1)}, bf16[16,6144]{1,0:T(8,128)(2,1)S(1)}, u32[]{:S(2)}, u32[]{:S(2)}) %collective-permute-start.21) | collective-permute-done | bytes 196640 | tf_op jit(solution)/shard_map/ppermute | solution.py:40
  95.1 4.3 %collective-permute-start.22 = (bf16[16,6144]{1,0:T(8,128)(2,1)S(1)}, bf16[16,6144]{1,0:T(8,128)(2,1)S(1)}, u32[]{:S(2)}, u32[]{:S(2)}) collective-permute-start(bf16[16,6144]{1,0:T(8,128)(2,1)S(1)} %fusion), channel_id=1, source_target_pairs={{0,4},{1,5},{2,6},{3,7},{4,0},{5,1},{6,2},{7,3},{8,12},{9,13},{10,... | collective-permute-start | bytes 589832 | tf_op jit(solution)/shard_map/ppermute | solution.py:40
  99.4 5.7 %collective-permute-done.22 = bf16[16,6144]{1,0:T(8,128)(2,1)S(1)} collective-permute-done((bf16[16,6144]{1,0:T(8,128)(2,1)S(1)}, bf16[16,6144]{1,0:T(8,128)(2,1)S(1)}, u32[]{:S(2)}, u32[]{:S(2)}) %collective-permute-start.22) | collective-permute-done | bytes 196640 | tf_op jit(solution)/shard_map/ppermute | solution.py:40
  105.2 0.8 add_convert_fusion
  (42 shorter events, 0.9 us)
Async XLA Ops:
  1.8 7.1 %collective-permute-start = (bf16[16,6272]{1,0:T(8,128)(2,1)}, bf16[16,6272]{1,0:T(8,128)(2,1)S(1)}, u32[]{:S(2)}, u32[]{:S(2)}) collective-permute-start(bf16[16,6272]{1,0:T(8,128)(2,1)} %prepare.1), channel_id=1, source_target_pairs={{0,1},{1,0},{2,3},{3,2},{4,5},{5,4},{6,7},{7,6},{8,24},{9,25},{10,... | collective-permute-start | bytes 602120 | tf_op jit(solution)/shard_map/ppermute | solution.py:40
  4.8 12.0 %collective-permute-start.5 = (bf16[16,6272]{1,0:T(8,128)(2,1)}, bf16[16,6272]{1,0:T(8,128)(2,1)S(1)}, u32[]{:S(2)}, u32[]{:S(2)}) collective-permute-start(bf16[16,6272]{1,0:T(8,128)(2,1)} %prepare.1), channel_id=1, source_target_pairs={{0,4},{1,5},{2,6},{3,7},{4,0},{5,1},{6,2},{7,3},{8,12},{9,13},{10,... | collective-permute-start | bytes 602120 | tf_op jit(solution)/shard_map/ppermute | solution.py:40
  7.4 11.6 %collective-permute-start.2 = (bf16[16,6272]{1,0:T(8,128)(2,1)}, bf16[16,6272]{1,0:T(8,128)(2,1)S(1)}, u32[]{:S(2)}, u32[]{:S(2)}) collective-permute-start(bf16[16,6272]{1,0:T(8,128)(2,1)} %prepare.1), channel_id=1, source_target_pairs={{0,2},{1,3},{2,0},{3,1},{4,6},{5,7},{6,4},{7,5},{8,10},{9,11},{10,... | collective-permute-start | bytes 602120 | tf_op jit(solution)/shard_map/ppermute | solution.py:40
  9.0 36.1 %copy-start = (bf16[1,6144,1024]{2,1,0:T(8,128)(2,1)S(1)}, bf16[1,6144,1024]{2,1,0:T(8,128)(2,1)}, u32[]{:S(2)}) copy-start(bf16[1,6144,1024]{2,1,0:T(8,128)(2,1)} %refs_4_.1) | copy-start | bytes 37748740
  10.1 25.9 %collective-permute-start.1 = (bf16[32,6272]{1,0:T(8,128)(2,1)S(1)}, bf16[32,6272]{1,0:T(8,128)(2,1)S(1)}, u32[]{:S(2)}, u32[]{:S(2)}) collective-permute-start(bf16[32,6272]{1,0:T(8,128)(2,1)S(1)} %pad_maximum_fusion.1), channel_id=1, source_target_pairs={{0,16},{1,17},{2,18},{3,19},{4,20},{5,21},{6,22},{7,23},{8,9},{9,8... | collective-permute-start | bytes 1204232 | tf_op jit(solution)/shard_map/ppermute | solution.py:40
  16.8 9.9 %collective-permute-start.8 = (bf16[16,6272]{1,0:T(8,128)(2,1)S(1)}, bf16[16,6272]{1,0:T(8,128)(2,1)S(1)}, u32[]{:S(2)}, u32[]{:S(2)}) collective-permute-start(bf16[16,6272]{1,0:T(8,128)(2,1)S(1)} %collective-permute-done.5), channel_id=1, source_target_pairs={{0,2},{1,3},{2,0},{3,1},{4,6},{5,7},{6,4},{7,5},{8,10},{9,11},{10,... | collective-permute-start | bytes 602120 | tf_op jit(solution)/shard_map/ppermute | solution.py:40
  17.5 5.7 %collective-permute-start.6 = (bf16[16,6272]{1,0:T(8,128)(2,1)S(1)}, bf16[16,6272]{1,0:T(8,128)(2,1)S(1)}, u32[]{:S(2)}, u32[]{:S(2)}) collective-permute-start(bf16[16,6272]{1,0:T(8,128)(2,1)S(1)} %collective-permute-done.5), channel_id=1, source_target_pairs={{0,1},{1,0},{2,3},{3,2},{4,5},{5,4},{6,7},{7,6},{8,24},{9,25},{10,... | collective-permute-start | bytes 602120 | tf_op jit(solution)/shard_map/ppermute | solution.py:40
  19.0 6.9 %collective-permute-start.3 = (bf16[16,6272]{1,0:T(8,128)(2,1)S(1)}, bf16[16,6272]{1,0:T(8,128)(2,1)S(1)}, u32[]{:S(2)}, u32[]{:S(2)}) collective-permute-start(bf16[16,6272]{1,0:T(8,128)(2,1)S(1)} %collective-permute-done.2), channel_id=1, source_target_pairs={{0,1},{1,0},{2,3},{3,2},{4,5},{5,4},{6,7},{7,6},{8,24},{9,25},{10,... | collective-permute-start | bytes 602120 | tf_op jit(solution)/shard_map/ppermute | solution.py:40
  23.2 13.8 %collective-permute-start.7 = (bf16[32,6272]{1,0:T(8,128)(2,1)S(1)}, bf16[32,6272]{1,0:T(8,128)(2,1)S(1)}, u32[]{:S(2)}, u32[]{:S(2)}) collective-permute-start(bf16[32,6272]{1,0:T(8,128)(2,1)S(1)} %pad_maximum_fusion.3), channel_id=1, source_target_pairs={{0,16},{1,17},{2,18},{3,19},{4,20},{5,21},{6,22},{7,23},{8,9},{9,8... | collective-permute-start | bytes 1204232 | tf_op jit(solution)/shard_map/ppermute | solution.py:40
  25.9 11.7 %collective-permute-start.4 = (bf16[32,6272]{1,0:T(8,128)(2,1)S(1)}, bf16[32,6272]{1,0:T(8,128)(2,1)S(1)}, u32[]{:S(2)}, u32[]{:S(2)}) collective-permute-start(bf16[32,6272]{1,0:T(8,128)(2,1)S(1)} %pad_maximum_fusion.2), channel_id=1, source_target_pairs={{0,16},{1,17},{2,18},{3,19},{4,20},{5,21},{6,22},{7,23},{8,9},{9,8... | collective-permute-start | bytes 1204232 | tf_op jit(solution)/shard_map/ppermute | solution.py:40
  26.7 7.9 %collective-permute-start.9 = (bf16[16,6272]{1,0:T(8,128)(2,1)S(1)}, bf16[16,6272]{1,0:T(8,128)(2,1)S(1)}, u32[]{:S(2)}, u32[]{:S(2)}) collective-permute-start(bf16[16,6272]{1,0:T(8,128)(2,1)S(1)} %collective-permute-done.8), channel_id=1, source_target_pairs={{0,1},{1,0},{2,3},{3,2},{4,5},{5,4},{6,7},{7,6},{8,24},{9,25},{10,... | collective-permute-start | bytes 602120 | tf_op jit(solution)/shard_map/ppermute | solution.py:40
  34.6 7.9 %collective-permute-start.10 = (bf16[32,6272]{1,0:T(8,128)(2,1)S(1)}, bf16[32,6272]{1,0:T(8,128)(2,1)S(1)}, u32[]{:S(2)}, u32[]{:S(2)}) collective-permute-start(bf16[32,6272]{1,0:T(8,128)(2,1)S(1)} %pad_maximum_fusion.4), channel_id=1, source_target_pairs={{0,16},{1,17},{2,18},{3,19},{4,20},{5,21},{6,22},{7,23},{8,9},{9,8... | collective-permute-start | bytes 1204232 | tf_op jit(solution)/shard_map/ppermute | solution.py:40
  38.8 6.2 %collective-permute-start.11 = (bf16[96,6144]{1,0:T(8,128)(2,1)S(1)}, bf16[96,6144]{1,0:T(8,128)(2,1)S(1)}, u32[]{:S(2)}, u32[]{:S(2)}) collective-permute-start(bf16[96,6144]{1,0:T(8,128)(2,1)S(1)} %get-tuple-element.19), channel_id=1, source_target_pairs={{0,8},{1,9},{2,10},{3,11},{4,12},{5,13},{6,14},{7,15},{8,0},{9,1},... | collective-permute-start | bytes 3538952 | tf_op jit(solution)/shard_map/ppermute | solution.py:40
  43.2 1.8 %collective-permute-start.12 = (bf16[32,6144]{1,0:T(8,128)(2,1)S(1)}, bf16[32,6144]{1,0:T(8,128)(2,1)S(1)}, u32[]{:S(2)}, u32[]{:S(2)}) collective-permute-start(bf16[32,6144]{1,0:T(8,128)(2,1)S(1)} %get-tuple-element.20), channel_id=1, source_target_pairs={{0,8},{1,9},{2,10},{3,11},{4,12},{5,13},{6,14},{7,15},{8,0},{9,1},... | collective-permute-start | bytes 1179656 | tf_op jit(solution)/shard_map/ppermute | solution.py:40
  56.2 2.4 %collective-permute-start.13 = (bf16[64,6144]{1,0:T(8,128)(2,1)S(1)}, bf16[64,6144]{1,0:T(8,128)(2,1)S(1)}, u32[]{:S(2)}, u32[]{:S(2)}) collective-permute-start(bf16[64,6144]{1,0:T(8,128)(2,1)S(1)} %get-tuple-element.22), channel_id=1, source_target_pairs={{0,8},{1,9},{2,10},{3,11},{4,12},{5,13},{6,14},{7,15},{8,0},{9,1},... | collective-permute-start | bytes 2359304 | tf_op jit(solution)/shard_map/ppermute | solution.py:40
  56.4 5.7 %collective-permute-start.16 = (bf16[64,6144]{1,0:T(8,128)(2,1)S(1)}, bf16[64,6144]{1,0:T(8,128)(2,1)S(1)}, u32[]{:S(2)}, u32[]{:S(2)}) collective-permute-start(bf16[64,6144]{1,0:T(8,128)(2,1)S(1)} %get-tuple-element.25), channel_id=1, source_target_pairs={{0,8},{1,9},{2,10},{3,11},{4,12},{5,13},{6,14},{7,15},{8,0},{9,1},... | collective-permute-start | bytes 2359304 | tf_op jit(solution)/shard_map/ppermute | solution.py:40
  59.9 7.8 %collective-permute-start.23 = (bf16[32,6144]{1,0:T(8,128)(2,1)S(1)}, bf16[32,6144]{1,0:T(8,128)(2,1)S(1)}, u32[]{:S(2)}, u32[]{:S(2)}) collective-permute-start(bf16[32,6144]{1,0:T(8,128)(2,1)S(1)} %slice.61), channel_id=1, source_target_pairs={{0,16},{1,17},{2,18},{3,19},{4,20},{5,21},{6,22},{7,23},{8,9},{9,8... | collective-permute-start | bytes 1179656 | tf_op jit(solution)/shard_map/ppermute | solution.py:40
  61.3 12.9 %collective-permute-start.14 = (bf16[32,6144]{1,0:T(8,128)(2,1)S(1)}, bf16[32,6144]{1,0:T(8,128)(2,1)S(1)}, u32[]{:S(2)}, u32[]{:S(2)}) collective-permute-start(bf16[32,6144]{1,0:T(8,128)(2,1)S(1)} %slice.49), channel_id=1, source_target_pairs={{0,16},{1,17},{2,18},{3,19},{4,20},{5,21},{6,22},{7,23},{8,9},{9,8... | collective-permute-start | bytes 1179656 | tf_op jit(solution)/shard_map/ppermute | solution.py:40
  63.4 17.0 %collective-permute-start.19 = (bf16[32,6144]{1,0:T(8,128)(2,1)S(1)}, bf16[32,6144]{1,0:T(8,128)(2,1)S(1)}, u32[]{:S(2)}, u32[]{:S(2)}) collective-permute-start(bf16[32,6144]{1,0:T(8,128)(2,1)S(1)} %slice.57), channel_id=1, source_target_pairs={{0,16},{1,17},{2,18},{3,19},{4,20},{5,21},{6,22},{7,23},{8,9},{9,8... | collective-permute-start | bytes 1179656 | tf_op jit(solution)/shard_map/ppermute | solution.py:40
  64.8 22.0 %collective-permute-start.17 = (bf16[32,6144]{1,0:T(8,128)(2,1)S(1)}, bf16[32,6144]{1,0:T(8,128)(2,1)S(1)}, u32[]{:S(2)}, u32[]{:S(2)}) collective-permute-start(bf16[32,6144]{1,0:T(8,128)(2,1)S(1)} %slice.53), channel_id=1, source_target_pairs={{0,16},{1,17},{2,18},{3,19},{4,20},{5,21},{6,22},{7,23},{8,9},{9,8... | collective-permute-start | bytes 1179656 | tf_op jit(solution)/shard_map/ppermute | solution.py:40
  67.8 22.2 %collective-permute-start.24 = (bf16[16,6144]{1,0:T(8,128)(2,1)S(1)}, bf16[16,6144]{1,0:T(8,128)(2,1)S(1)}, u32[]{:S(2)}, u32[]{:S(2)}) collective-permute-start(bf16[16,6144]{1,0:T(8,128)(2,1)S(1)} %slice.71), channel_id=1, source_target_pairs={{0,1},{1,0},{2,3},{3,2},{4,5},{5,4},{6,7},{7,6},{8,24},{9,25},{10,... | collective-permute-start | bytes 589832 | tf_op jit(solution)/shard_map/ppermute | solution.py:40
  74.2 25.2 %collective-permute-start.15 = (bf16[16,6144]{1,0:T(8,128)(2,1)S(1)}, bf16[16,6144]{1,0:T(8,128)(2,1)S(1)}, u32[]{:S(2)}, u32[]{:S(2)}) collective-permute-start(bf16[16,6144]{1,0:T(8,128)(2,1)S(1)} %slice.65), channel_id=1, source_target_pairs={{0,1},{1,0},{2,3},{3,2},{4,5},{5,4},{6,7},{7,6},{8,24},{9,25},{10,... | collective-permute-start | bytes 589832 | tf_op jit(solution)/shard_map/ppermute | solution.py:40
  80.6 7.6 %collective-permute-start.20 = (bf16[16,6144]{1,0:T(8,128)(2,1)S(1)}, bf16[16,6144]{1,0:T(8,128)(2,1)S(1)}, u32[]{:S(2)}, u32[]{:S(2)}) collective-permute-start(bf16[16,6144]{1,0:T(8,128)(2,1)S(1)} %slice.69), channel_id=1, source_target_pairs={{0,1},{1,0},{2,3},{3,2},{4,5},{5,4},{6,7},{7,6},{8,24},{9,25},{10,... | collective-permute-start | bytes 589832 | tf_op jit(solution)/shard_map/ppermute | solution.py:40
  86.9 5.7 %collective-permute-start.18 = (bf16[16,6144]{1,0:T(8,128)(2,1)S(1)}, bf16[16,6144]{1,0:T(8,128)(2,1)S(1)}, u32[]{:S(2)}, u32[]{:S(2)}) collective-permute-start(bf16[16,6144]{1,0:T(8,128)(2,1)S(1)} %slice.67), channel_id=1, source_target_pairs={{0,1},{1,0},{2,3},{3,2},{4,5},{5,4},{6,7},{7,6},{8,24},{9,25},{10,... | collective-permute-start | bytes 589832 | tf_op jit(solution)/shard_map/ppermute | solution.py:40
  88.2 6.9 %collective-permute-start.21 = (bf16[16,6144]{1,0:T(8,128)(2,1)S(1)}, bf16[16,6144]{1,0:T(8,128)(2,1)S(1)}, u32[]{:S(2)}, u32[]{:S(2)}) collective-permute-start(bf16[16,6144]{1,0:T(8,128)(2,1)S(1)} %slice_add_fusion.5), channel_id=1, source_target_pairs={{0,2},{1,3},{2,0},{3,1},{4,6},{5,7},{6,4},{7,5},{8,10},{9,11},{10,... | collective-permute-start | bytes 589832 | tf_op jit(solution)/shard_map/ppermute | solution.py:40
  90.0 9.4 %collective-permute-start.25 = (bf16[16,6144]{1,0:T(8,128)(2,1)S(1)}, bf16[16,6144]{1,0:T(8,128)(2,1)S(1)}, u32[]{:S(2)}, u32[]{:S(2)}) collective-permute-start(bf16[16,6144]{1,0:T(8,128)(2,1)S(1)} %slice_add_fusion.4), channel_id=1, source_target_pairs={{0,2},{1,3},{2,0},{3,1},{4,6},{5,7},{6,4},{7,5},{8,10},{9,11},{10,... | collective-permute-start | bytes 589832 | tf_op jit(solution)/shard_map/ppermute | solution.py:40
  95.1 10.1 %collective-permute-start.22 = (bf16[16,6144]{1,0:T(8,128)(2,1)S(1)}, bf16[16,6144]{1,0:T(8,128)(2,1)S(1)}, u32[]{:S(2)}, u32[]{:S(2)}) collective-permute-start(bf16[16,6144]{1,0:T(8,128)(2,1)S(1)} %fusion), channel_id=1, source_target_pairs={{0,4},{1,5},{2,6},{3,7},{4,0},{5,1},{6,2},{7,3},{8,12},{9,13},{10,... | collective-permute-start | bytes 589832 | tf_op jit(solution)/shard_map/ppermute | solution.py:40

commit v3 on v2

--- a/solution.py
+++ b/solution.py
@@ -10,6 +10,7 @@
 
 CAP = 8
 META = 128
+SPLIT_OUT = (0,)
 FFT = 512
 OUT = 2048
 PLACE = 3072
@@ -63,8 +64,7 @@
         return [own] + [grid.move(own, grid.across_z(k)) for k in range(1, grid.z)]
     far = grid.move(own, grid.across_z(2))
     near = grid.move(own, grid.across_z(1))
-    last = grid.move(far, grid.across_z(1))
-    return [own, near, far, last]
+    return [own, near, far]
 
 
 def scatter_z(grid, parts):
@@ -80,20 +80,33 @@
     return (own.astype(f32) + far.astype(f32) + near.astype(f32)).astype(jnp.bfloat16)
 
 
-def spread(grid, block):
+def first_step(grid, block):
     firsts = [block] + [grid.move(block, grid.first(k)) for k in range(1, grid.x)]
-    half = jnp.concatenate(firsts, axis=0)
+    return jnp.concatenate(firsts, axis=0)
+
+
+def second_step(grid, half):
     seconds = [half] + [grid.move(half, grid.second(k)) for k in range(1, grid.y)]
     return jnp.concatenate(seconds, axis=0)
 
 
-def fold(grid, rows):
+def fold(grid, rows, at):
     size = rows.shape[0] // grid.y
-    moved = [grid.move(rows[k * size : (k + 1) * size], grid.second(-k)) for k in range(1, grid.y)]
-    half = sum(moved, rows[:size])
-    size = size // grid.x
-    moved = [grid.move(half[k * size : (k + 1) * size], grid.first(-k)) for k in range(1, grid.x)]
-    return sum(moved, half[:size])
+    one = size // grid.x
+    skip = one if at in SPLIT_OUT else 0
+    moved = [
+        grid.move(rows[k * size + skip : (k + 1) * size], grid.second(-k))
+        for k in range(1, grid.y)
+    ]
+    half = sum(moved, rows[skip:size])
+    moved = [
+        grid.move(half[k * one - skip : (k + 1) * one - skip], grid.first(-k))
+        for k in range(1, grid.x)
+    ]
+    if at not in SPLIT_OUT:
+        return sum(moved, half[:one])
+    moved += [grid.move(rows[k * size : k * size + one], grid.second(-k)) for k in range(1, grid.y)]
+    return sum([m.astype(jnp.float32) for m in moved], rows[:one].astype(jnp.float32))
 
 
 def prepare_kernel(tok_ref, gain_ref, ids_ref, slots_ref, route_ref, out_ref):
@@ -188,7 +201,7 @@
     gate, up_hbm, down_hbm = refs[:3]
     outs, refs = refs[3:7], refs[7:]
     up, down, gated, hidden, up_sems, down_sems = refs
-    width, some = gate.shape[2], outs[0].shape[0]
+    width = gate.shape[2]
     up_tiles, down_tiles = width // FFT, features // OUT
 
     def piece():
@@ -228,13 +241,46 @@
         place = tile(i, OUT)
         product = jnp.dot(hidden[...], down[:, place], preferred_element_type=f32)
         product = product.astype(bf16)
-        for at, out in enumerate(outs):
-            out[:, place] = product[at * some : (at + 1) * some]
+        at = 0
+        for out in outs:
+            out[:, place] = product[at : at + out.shape[0]]
+            at += out.shape[0]
+
+
+def fetch_kernel(source, target, sems):
+    count = sems.shape[0]
+    size = source.shape[1] // count
+    copies = [
+        pltpu.make_async_copy(
+            source.at[:, pl.ds(i * size, size)], target.at[:, pl.ds(i * size, size)], sems.at[i]
+        )
+        for i in range(count)
+    ]
+    for copy in copies:
+        copy.start()
+    for copy in copies:
+        copy.wait()
+
+
+def fetch(weights):
+    return pl.pallas_call(
+        fetch_kernel,
+        out_shape=jax.ShapeDtypeStruct(weights.shape, weights.dtype),
+        in_specs=[pl.BlockSpec(memory_space=pltpu.HBM)],
+        out_specs=pl.BlockSpec(memory_space=pltpu.VMEM),
+        scratch_shapes=[pltpu.SemaphoreType.DMA((8,))],
+        cost_estimate=pl.CostEstimate(
+            flops=0, bytes_accessed=2 * weights.size * 2, transcendentals=0
+        ),
+        compiler_params=pltpu.CompilerParams(vmem_limit_bytes=2**20),
+        name="fetch",
+    )(weights)
 
 
 def ffn(mine, theirs, w_gate, w_up, w_down):
     bf16 = jnp.bfloat16
     each, features = sum(m.shape[0] for m in mine), mine[0].shape[1]
+    lengths = [m.shape[0] for m in mine]
     width = w_gate.shape[2]
     need = 2 * (3 * features * width + 4 * each * features + 2 * each * width)
     if need > 56 * 2**20 or width % FFT or features % OUT:
@@ -243,11 +289,13 @@
         up_proj = jnp.dot(piece, w_up[0], preferred_element_type=jnp.float32)
         hidden = (jax.nn.silu(gate_proj) * up_proj).astype(bf16)
         product = jnp.dot(hidden, w_down[0], preferred_element_type=jnp.float32).astype(bf16)
-        return [product[at * each // 2 : (at + 1) * each // 2] for at in range(4)]
+        cuts = [0, lengths[0], each, each + lengths[0], 2 * each]
+        return [product[a:b] for a, b in zip(cuts, cuts[1:])]
+    w_gate = fetch(w_gate)
     vmem, hbm = pl.BlockSpec(memory_space=pltpu.VMEM), pl.BlockSpec(memory_space=pltpu.HBM)
     return pl.pallas_call(
         functools.partial(ffn_kernel, features, len(mine + theirs)),
-        out_shape=[jax.ShapeDtypeStruct((each // 2, features), bf16)] * 4,
+        out_shape=[jax.ShapeDtypeStruct((length, features), bf16) for length in 2 * lengths],
         in_specs=[vmem] * (len(mine + theirs) + 1) + [hbm] * 2,
         out_specs=[vmem] * 4,
         scratch_shapes=[
@@ -317,7 +365,10 @@
 def local(grid, tokens, norm_gain, expert_ids, slot_ids, route_weights, w_gate, w_up, w_down):
     tok_rows, features = tokens.shape
     own = prepare(tokens, norm_gain, expert_ids, slot_ids, route_weights)
-    groups = [spread(grid, block) for block in gather_z(grid, own)]
+    halves = [first_step(grid, block) for block in gather_z(grid, own)]
+    if len(halves) < grid.z:
+        halves.append(grid.move(halves[2], grid.across_z(1)))
+    groups = [second_step(grid, half) for half in halves]
     mine, theirs = [], []
     for some in (groups[:-1], groups[-1:]):
         kept, away = place_rows(some, tok_rows, features)
@@ -328,12 +379,11 @@
     for side in (1, 0):
         moved[side] = grid.move(results[2 + side], grid.sibling)
     parts = [None] * grid.z
-    some = grid.z // 2
     for side in (1, 0):
-        held = groups[side * some : (side + 1) * some]
-        mixed = mix(held, results[side], moved[side], tok_rows)
-        for k in reversed(range(some)):
-            parts[side * some + k] = fold(grid, mixed[k])
+        held = list(range(grid.z))[-1:] if side else list(range(grid.z))[:-1]
+        mixed = mix([groups[k] for k in held], results[side], moved[side], tok_rows)
+        for k in reversed(held):
+            parts[k] = fold(grid, mixed[k - held[0]], k)
     return scatter_z(grid, parts)
 
 

time: 106 us -> 114 us (1.075)
  local copies, waits for them, and re-layouts: 0.38 us -> 4.94 us
  waiting for transfers between devices: 52.3 us -> 56.5 us
    unnamed x8, local copies, waits for them, and re-layouts: 0.11 us -> 4.66 us
    ppermute x26, waiting for transfers between devices: 52.3 us -> 56.5 us  [move(): return lax.ppermute(value, AXES, pairs)]
  transfers between devices with their start and end apart: 26 -> 26, of which waited for: 15 -> 12; matrix products, arithmetic and copies ran while one was open for 3% -> 1% of each run, Pallas kernels for 4% -> 4%
where the time goes in v3:
time: 114 us
  waiting for transfers between devices  56.5 us (50%)
  starting transfers between devices  31.8 us (28%)
  Pallas kernels  18.4 us (16%)
  local copies, waits for them, and re-layouts  4.94 us (4%)
  other arithmetic  2.14 us (2%)
    ppermute x26, waiting for transfers between devices, move(): return lax.ppermute(value, AXES, pairs)  56.5 us
    ppermute x26, starting transfers between devices, move(): return lax.ppermute(value, AXES, pairs)  31.8 us
    pallas_call x1, Pallas kernels, ffn(): pl.pallas_call(functools.partial(ffn_kernel, features, len(mine + theirs)...  11.2 us
    unnamed x8, local copies, waits for them, and re-layouts  4.66 us
    pallas_call x2, Pallas kernels, mix(): pl.pallas_call(functools.partial(mix_kernel, n, tok_rows, features), grid...  2.56 us
  transfers between devices with their start and end apart: 26, of which 12 were waited for; matrix products, arithmetic and copies ran while one was open for 1% of the time, Pallas kernels for 4%

profile of v3, /device:TPU:0, one launch (start us, length us, event | category | flops | bytes accessed | tf_op | source)
XLA Modules:
  0.0 114.1 jit_solution(16007705981754315123)
XLA Ops:
  0.0 1.8 %prepare.1 = bf16[16,6272]{1,0:T(8,128)(2,1)} custom-call(bf16[16,6144]{1,0:T(8,128)(2,1)} %tok_ref.1, bf16[48,128]{1,0:T(8,128)(2,1)} %bitcast.4, s32[2,16]{1,0:T(2,128)} %bitcast.5, s32[2,16]{1,0:T(2,128)} %bitcast.6, f32[2,16]{1,0:T(2,128)} %bitcast.7), custom_call_target="tpu_custom_call" | custom-call | tf_op jit(solution)/shard_map/prepare/pallas_call | solution.py:140
  1.8 3.0 %collective-permute-start = (bf16[16,6272]{1,0:T(8,128)(2,1)}, bf16[16,6272]{1,0:T(8,128)(2,1)S(1)}, u32[]{:S(2)}, u32[]{:S(2)}) collective-permute-start(bf16[16,6272]{1,0:T(8,128)(2,1)} %prepare.1), channel_id=1, source_target_pairs={{0,1},{1,0},{2,3},{3,2},{4,5},{5,4},{6,7},{7,6},{8,24},{9,25},{10,... | collective-permute-start | bytes 602120 | tf_op jit(solution)/shard_map/ppermute | solution.py:41
  4.8 2.6 %collective-permute-start.5 = (bf16[16,6272]{1,0:T(8,128)(2,1)}, bf16[16,6272]{1,0:T(8,128)(2,1)S(1)}, u32[]{:S(2)}, u32[]{:S(2)}) collective-permute-start(bf16[16,6272]{1,0:T(8,128)(2,1)} %prepare.1), channel_id=1, source_target_pairs={{0,4},{1,5},{2,6},{3,7},{4,0},{5,1},{6,2},{7,3},{8,12},{9,13},{10,... | collective-permute-start | bytes 602120 | tf_op jit(solution)/shard_map/ppermute | solution.py:41
  7.4 1.6 %collective-permute-start.2 = (bf16[16,6272]{1,0:T(8,128)(2,1)}, bf16[16,6272]{1,0:T(8,128)(2,1)S(1)}, u32[]{:S(2)}, u32[]{:S(2)}) collective-permute-start(bf16[16,6272]{1,0:T(8,128)(2,1)} %prepare.1), channel_id=1, source_target_pairs={{0,2},{1,3},{2,0},{3,1},{4,6},{5,7},{6,4},{7,5},{8,10},{9,11},{10,... | collective-permute-start | bytes 602120 | tf_op jit(solution)/shard_map/ppermute | solution.py:41
  9.0 1.0 pad_maximum_fusion.1
  10.0 1.8 %collective-permute-start.1 = (bf16[32,6272]{1,0:T(8,128)(2,1)S(1)}, bf16[32,6272]{1,0:T(8,128)(2,1)S(1)}, u32[]{:S(2)}, u32[]{:S(2)}) collective-permute-start(bf16[32,6272]{1,0:T(8,128)(2,1)S(1)} %pad_maximum_fusion.1), channel_id=1, source_target_pairs={{0,16},{1,17},{2,18},{3,19},{4,20},{5,21},{6,22},{7,23},{8,9},{9,8... | collective-permute-start | bytes 1204232 | tf_op jit(solution)/shard_map/ppermute | solution.py:41
  11.8 5.0 %collective-permute-done.5 = bf16[16,6272]{1,0:T(8,128)(2,1)S(1)} collective-permute-done((bf16[16,6272]{1,0:T(8,128)(2,1)}, bf16[16,6272]{1,0:T(8,128)(2,1)S(1)}, u32[]{:S(2)}, u32[]{:S(2)}) %collective-permute-start.5) | collective-permute-done | bytes 200736 | tf_op jit(solution)/shard_map/ppermute | solution.py:41
  16.8 1.5 %collective-permute-start.6 = (bf16[16,6272]{1,0:T(8,128)(2,1)S(1)}, bf16[16,6272]{1,0:T(8,128)(2,1)S(1)}, u32[]{:S(2)}, u32[]{:S(2)}) collective-permute-start(bf16[16,6272]{1,0:T(8,128)(2,1)S(1)} %collective-permute-done.5), channel_id=1, source_target_pairs={{0,1},{1,0},{2,3},{3,2},{4,5},{5,4},{6,7},{7,6},{8,24},{9,25},{10,... | collective-permute-start | bytes 602120 | tf_op jit(solution)/shard_map/ppermute | solution.py:41
  18.3 0.6 collective-permute-start.3
  19.0 3.6 %collective-permute-done.6 = bf16[16,6272]{1,0:T(8,128)(2,1)S(1)} collective-permute-done((bf16[16,6272]{1,0:T(8,128)(2,1)S(1)}, bf16[16,6272]{1,0:T(8,128)(2,1)S(1)}, u32[]{:S(2)}, u32[]{:S(2)}) %collective-permute-start.6) | collective-permute-done | bytes 200736 | tf_op jit(solution)/shard_map/ppermute | solution.py:41
  22.6 0.7 collective-permute-start.8
  23.3 0.5 collective-permute-start.7
  23.8 0.9 collective-permute-done.3
  24.7 0.7 collective-permute-start.4
  25.5 9.9 %collective-permute-done.4 = bf16[32,6272]{1,0:T(8,128)(2,1)S(1)} collective-permute-done((bf16[32,6272]{1,0:T(8,128)(2,1)S(1)}, bf16[32,6272]{1,0:T(8,128)(2,1)S(1)}, u32[]{:S(2)}, u32[]{:S(2)}) %collective-permute-start.4) | collective-permute-done | bytes 401440 | tf_op jit(solution)/shard_map/ppermute | solution.py:41
  35.5 1.2 %place.2 = (bf16[96,6144]{1,0:T(8,128)(2,1)S(1)}, bf16[96,6144]{1,0:T(8,128)(2,1)S(1)}) custom-call(bf16[64,6272]{1,0:T(8,128)(2,1)S(1)} %pad_maximum_fusion.refs_0_, bf16[64,6272]{1,0:T(8,128)(2,1)S(1)} %constant_dynamic-update-slice_fusion.refs_1_, bf16[64,6272]{1,0:T(8,128)(2,1)S(1)} %constant_dynamic-update-slice_fusion.5.refs_2_), custom_call_target="tpu_custom_call" | custom-call | flops 452984832 | bytes 4718592 | tf_op jit(solution)/shard_map/place/pallas_call | solution.py:185
  36.7 0.1 collective-permute-start.10
  36.8 0.6 collective-permute-start.9
  37.4 7.3 %collective-permute-done.9 = bf16[32,6272]{1,0:T(8,128)(2,1)S(1)} collective-permute-done((bf16[32,6272]{1,0:T(8,128)(2,1)S(1)}, bf16[32,6272]{1,0:T(8,128)(2,1)S(1)}, u32[]{:S(2)}, u32[]{:S(2)}) %collective-permute-start.9) | collective-permute-done | bytes 401440 | tf_op jit(solution)/shard_map/ppermute | solution.py:41
  44.8 0.6 place.3
  45.4 0.1 collective-permute-start.11
  45.5 4.6 %copy-done = bf16[1,6144,1024]{2,1,0:T(8,128)(2,1)S(1)} copy-done((bf16[1,6144,1024]{2,1,0:T(8,128)(2,1)S(1)}, bf16[1,6144,1024]{2,1,0:T(8,128)(2,1)}, u32[]{:S(2)}) %copy-start) | copy-done | bytes 12582936
  50.1 0.9 fetch.1.refs_4_
  51.1 11.2 %ffn.1 = (bf16[96,6144]{1,0:T(8,128)(2,1)S(1)}, bf16[32,6144]{1,0:T(8,128)(2,1)S(1)}, bf16[96,6144]{1,0:T(8,128)(2,1)S(1)}, bf16[32,6144]{1,0:T(8,128)(2,1)S(1)}) custom-call(bf16[96,6144]{1,0:T(8,128)(2,1)S(1)} %get-tuple-element.16.refs_0_, bf16[32,6144]{1,0:T(8,128)(2,1)S(1)} %get-tuple-element.17.refs_1_, ...), custom_call_target="tpu_custom_call" | custom-call | flops 9663676416 | bytes 37748736 | tf_op jit(solution)/shard_map/ffn/pallas_call | solution.py:296
  62.3 0.6 collective-permute-start.18
  62.8 1.3 %collective-permute-done.18.refs_2_ = bf16[32,6144]{1,0:T(8,128)(2,1)S(1)} collective-permute-done((bf16[32,6144]{1,0:T(8,128)(2,1)S(1)}, bf16[32,6144]{1,0:T(8,128)(2,1)S(1)}, u32[]{:S(2)}, u32[]{:S(2)}) %collective-permute-start.18) | collective-permute-done | bytes 393248 | tf_op jit(solution)/shard_map/ppermute | solution.py:41
  64.2 0.8 mix.3
  65.0 0.6 collective-permute-start.19
  65.6 1.1 collective-permute-start.12
  66.7 6.2 %collective-permute-done.19 = bf16[32,6144]{1,0:T(8,128)(2,1)S(1)} collective-permute-done((bf16[32,6144]{1,0:T(8,128)(2,1)S(1)}, bf16[32,6144]{1,0:T(8,128)(2,1)S(1)}, u32[]{:S(2)}, u32[]{:S(2)}) %collective-permute-start.19) | collective-permute-done | bytes 393248 | tf_op jit(solution)/shard_map/ppermute | solution.py:41
  73.0 1.6 %collective-permute-start.20 = (bf16[16,6144]{1,0:T(8,128)(2,1)S(1)}, bf16[16,6144]{1,0:T(8,128)(2,1)S(1)}, u32[]{:S(2)}, u32[]{:S(2)}) collective-permute-start(bf16[16,6144]{1,0:T(8,128)(2,1)S(1)} %slice.69), channel_id=1, source_target_pairs={{0,1},{1,0},{2,3},{3,2},{4,5},{5,4},{6,7},{7,6},{8,24},{9,25},{10,... | collective-permute-start | bytes 589832 | tf_op jit(solution)/shard_map/ppermute | solution.py:41
  74.5 1.7 %mix.2 = (bf16[64,6144]{1,0:T(8,128)(2,1)S(1)}, bf16[64,6144]{1,0:T(8,128)(2,1)S(1)}, bf16[64,6144]{1,0:T(8,128)(2,1)S(1)}) custom-call(bf16[64,6272]{1,0:T(8,128)(2,1)S(1)} %pad_maximum_fusion.refs_0_, bf16[64,6272]{1,0:T(8,128)(2,1)S(1)} %constant_dynamic-update-slice_fusion.refs_1_, bf16[64,6272]{1,0:T(8,128)(2,1)S(1)} %constant_dynamic-update-slice_fusion.5.refs_2_, ...), custom_call_target="tpu_custom_call" | custom-call | flops 905969664 | bytes 4718592 | tf_op jit(solution)/shard_map/mix/pallas_call | solution.py:349
  76.3 0.5 collective-permute-start.13
  76.8 3.4 %collective-permute-done.20 = bf16[16,6144]{1,0:T(8,128)(2,1)S(1)} collective-permute-done((bf16[16,6144]{1,0:T(8,128)(2,1)S(1)}, bf16[16,6144]{1,0:T(8,128)(2,1)S(1)}, u32[]{:S(2)}, u32[]{:S(2)}) %collective-permute-start.20) | collective-permute-done | bytes 196640 | tf_op jit(solution)/shard_map/ppermute | solution.py:41
  80.2 1.6 %collective-permute-start.21 = (bf16[16,6144]{1,0:T(8,128)(2,1)S(1)}, bf16[16,6144]{1,0:T(8,128)(2,1)S(1)}, u32[]{:S(2)}, u32[]{:S(2)}) collective-permute-start(bf16[16,6144]{1,0:T(8,128)(2,1)S(1)} %slice_add_fusion.4), channel_id=1, source_target_pairs={{0,2},{1,3},{2,0},{3,1},{4,6},{5,7},{6,4},{7,5},{8,10},{9,11},{10,... | collective-permute-start | bytes 589832 | tf_op jit(solution)/shard_map/ppermute | solution.py:41
  81.9 0.1 collective-permute-start.23
  82.0 2.0 %collective-permute-start.16 = (bf16[32,6144]{1,0:T(8,128)(2,1)S(1)}, bf16[32,6144]{1,0:T(8,128)(2,1)S(1)}, u32[]{:S(2)}, u32[]{:S(2)}) collective-permute-start(bf16[32,6144]{1,0:T(8,128)(2,1)S(1)} %slice.53), channel_id=1, source_target_pairs={{0,16},{1,17},{2,18},{3,19},{4,20},{5,21},{6,22},{7,23},{8,9},{9,8... | collective-permute-start | bytes 1179656 | tf_op jit(solution)/shard_map/ppermute | solution.py:41
  84.0 1.4 %collective-permute-start.14 = (bf16[16,6144]{1,0:T(8,128)(2,1)S(1)}, bf16[16,6144]{1,0:T(8,128)(2,1)S(1)}, u32[]{:S(2)}, u32[]{:S(2)}) collective-permute-start(bf16[16,6144]{1,0:T(8,128)(2,1)S(1)} %get-tuple-element.27), channel_id=1, source_target_pairs={{0,1},{1,0},{2,3},{3,2},{4,5},{5,4},{6,7},{7,6},{8,24},{9,25},{10,... | collective-permute-start | bytes 589832 | tf_op jit(solution)/shard_map/ppermute | solution.py:41
  85.4 0.1 collective-permute-start.15
  85.5 6.0 %collective-permute-done.23 = bf16[32,6144]{1,0:T(8,128)(2,1)S(1)} collective-permute-done((bf16[32,6144]{1,0:T(8,128)(2,1)S(1)}, bf16[32,6144]{1,0:T(8,128)(2,1)S(1)}, u32[]{:S(2)}, u32[]{:S(2)}) %collective-permute-start.23) | collective-permute-done | bytes 393248 | tf_op jit(solution)/shard_map/ppermute | solution.py:41
  91.6 1.6 %collective-permute-start.24 = (bf16[16,6144]{1,0:T(8,128)(2,1)S(1)}, bf16[16,6144]{1,0:T(8,128)(2,1)S(1)}, u32[]{:S(2)}, u32[]{:S(2)}) collective-permute-start(bf16[16,6144]{1,0:T(8,128)(2,1)S(1)} %slice.71), channel_id=1, source_target_pairs={{0,1},{1,0},{2,3},{3,2},{4,5},{5,4},{6,7},{7,6},{8,24},{9,25},{10,... | collective-permute-start | bytes 589832 | tf_op jit(solution)/shard_map/ppermute | solution.py:41
  93.2 4.7 %collective-permute-done.16 = bf16[32,6144]{1,0:T(8,128)(2,1)S(1)} collective-permute-done((bf16[32,6144]{1,0:T(8,128)(2,1)S(1)}, bf16[32,6144]{1,0:T(8,128)(2,1)S(1)}, u32[]{:S(2)}, u32[]{:S(2)}) %collective-permute-start.16) | collective-permute-done | bytes 393248 | tf_op jit(solution)/shard_map/ppermute | solution.py:41
  98.0 1.5 %collective-permute-start.17 = (bf16[16,6144]{1,0:T(8,128)(2,1)S(1)}, bf16[16,6144]{1,0:T(8,128)(2,1)S(1)}, u32[]{:S(2)}, u32[]{:S(2)}) collective-permute-start(bf16[16,6144]{1,0:T(8,128)(2,1)S(1)} %slice.65), channel_id=1, source_target_pairs={{0,1},{1,0},{2,3},{3,2},{4,5},{5,4},{6,7},{7,6},{8,24},{9,25},{10,... | collective-permute-start | bytes 589832 | tf_op jit(solution)/shard_map/ppermute | solution.py:41
  99.5 1.9 %collective-permute-start.25 = (bf16[16,6144]{1,0:T(8,128)(2,1)S(1)}, bf16[16,6144]{1,0:T(8,128)(2,1)S(1)}, u32[]{:S(2)}, u32[]{:S(2)}) collective-permute-start(bf16[16,6144]{1,0:T(8,128)(2,1)S(1)} %slice_add_fusion.3), channel_id=1, source_target_pairs={{0,2},{1,3},{2,0},{3,1},{4,6},{5,7},{6,4},{7,5},{8,10},{9,11},{10,... | collective-permute-start | bytes 589832 | tf_op jit(solution)/shard_map/ppermute | solution.py:41
  101.4 2.3 %collective-permute-done.17 = bf16[16,6144]{1,0:T(8,128)(2,1)S(1)} collective-permute-done((bf16[16,6144]{1,0:T(8,128)(2,1)S(1)}, bf16[16,6144]{1,0:T(8,128)(2,1)S(1)}, u32[]{:S(2)}, u32[]{:S(2)}) %collective-permute-start.17) | collective-permute-done | bytes 196640 | tf_op jit(solution)/shard_map/ppermute | solution.py:41
  103.8 3.7 %collective-permute-start.22 = (bf16[16,6144]{1,0:T(8,128)(2,1)S(1)}, bf16[16,6144]{1,0:T(8,128)(2,1)S(1)}, u32[]{:S(2)}, u32[]{:S(2)}) collective-permute-start(bf16[16,6144]{1,0:T(8,128)(2,1)S(1)} %fusion), channel_id=1, source_target_pairs={{0,4},{1,5},{2,6},{3,7},{4,0},{5,1},{6,2},{7,3},{8,12},{9,13},{10,... | collective-permute-start | bytes 589832 | tf_op jit(solution)/shard_map/ppermute | solution.py:41
  107.5 5.7 %collective-permute-done.22 = bf16[16,6144]{1,0:T(8,128)(2,1)S(1)} collective-permute-done((bf16[16,6144]{1,0:T(8,128)(2,1)S(1)}, bf16[16,6144]{1,0:T(8,128)(2,1)S(1)}, u32[]{:S(2)}, u32[]{:S(2)}) %collective-permute-start.22) | collective-permute-done | bytes 196640 | tf_op jit(solution)/shard_map/ppermute | solution.py:41
  113.3 0.8 add_convert_fusion
  (41 shorter events, 0.8 us)
Async XLA Ops:
  1.8 7.1 %collective-permute-start = (bf16[16,6272]{1,0:T(8,128)(2,1)}, bf16[16,6272]{1,0:T(8,128)(2,1)S(1)}, u32[]{:S(2)}, u32[]{:S(2)}) collective-permute-start(bf16[16,6272]{1,0:T(8,128)(2,1)} %prepare.1), channel_id=1, source_target_pairs={{0,1},{1,0},{2,3},{3,2},{4,5},{5,4},{6,7},{7,6},{8,24},{9,25},{10,... | collective-permute-start | bytes 602120 | tf_op jit(solution)/shard_map/ppermute | solution.py:41
  4.8 12.0 %collective-permute-start.5 = (bf16[16,6272]{1,0:T(8,128)(2,1)}, bf16[16,6272]{1,0:T(8,128)(2,1)S(1)}, u32[]{:S(2)}, u32[]{:S(2)}) collective-permute-start(bf16[16,6272]{1,0:T(8,128)(2,1)} %prepare.1), channel_id=1, source_target_pairs={{0,4},{1,5},{2,6},{3,7},{4,0},{5,1},{6,2},{7,3},{8,12},{9,13},{10,... | collective-permute-start | bytes 602120 | tf_op jit(solution)/shard_map/ppermute | solution.py:41
  7.4 10.9 %collective-permute-start.2 = (bf16[16,6272]{1,0:T(8,128)(2,1)}, bf16[16,6272]{1,0:T(8,128)(2,1)S(1)}, u32[]{:S(2)}, u32[]{:S(2)}) collective-permute-start(bf16[16,6272]{1,0:T(8,128)(2,1)} %prepare.1), channel_id=1, source_target_pairs={{0,2},{1,3},{2,0},{3,1},{4,6},{5,7},{6,4},{7,5},{8,10},{9,11},{10,... | collective-permute-start | bytes 602120 | tf_op jit(solution)/shard_map/ppermute | solution.py:41
  10.0 15.5 %copy-start.1 = (bf16[16,6272]{1,0:T(8,128)(2,1)S(1)}, bf16[16,6272]{1,0:T(8,128)(2,1)}, u32[]{:S(2)}) copy-start(bf16[16,6272]{1,0:T(8,128)(2,1)} %prepare.1) | copy-start | bytes 602116
  10.0 15.5 %collective-permute-start.1 = (bf16[32,6272]{1,0:T(8,128)(2,1)S(1)}, bf16[32,6272]{1,0:T(8,128)(2,1)S(1)}, u32[]{:S(2)}, u32[]{:S(2)}) collective-permute-start(bf16[32,6272]{1,0:T(8,128)(2,1)S(1)} %pad_maximum_fusion.1), channel_id=1, source_target_pairs={{0,16},{1,17},{2,18},{3,19},{4,20},{5,21},{6,22},{7,23},{8,9},{9,8... | collective-permute-start | bytes 1204232 | tf_op jit(solution)/shard_map/ppermute | solution.py:41
  16.8 5.7 %collective-permute-start.6 = (bf16[16,6272]{1,0:T(8,128)(2,1)S(1)}, bf16[16,6272]{1,0:T(8,128)(2,1)S(1)}, u32[]{:S(2)}, u32[]{:S(2)}) collective-permute-start(bf16[16,6272]{1,0:T(8,128)(2,1)S(1)} %collective-permute-done.5), channel_id=1, source_target_pairs={{0,1},{1,0},{2,3},{3,2},{4,5},{5,4},{6,7},{7,6},{8,24},{9,25},{10,... | collective-permute-start | bytes 602120 | tf_op jit(solution)/shard_map/ppermute | solution.py:41
  18.3 6.3 %collective-permute-start.3 = (bf16[16,6272]{1,0:T(8,128)(2,1)S(1)}, bf16[16,6272]{1,0:T(8,128)(2,1)S(1)}, u32[]{:S(2)}, u32[]{:S(2)}) collective-permute-start(bf16[16,6272]{1,0:T(8,128)(2,1)S(1)} %collective-permute-done.2), channel_id=1, source_target_pairs={{0,1},{1,0},{2,3},{3,2},{4,5},{5,4},{6,7},{7,6},{8,24},{9,25},{10,... | collective-permute-start | bytes 602120 | tf_op jit(solution)/shard_map/ppermute | solution.py:41
  22.6 14.3 %collective-permute-start.8 = (bf16[32,6272]{1,0:T(8,128)(2,1)S(1)}, bf16[32,6272]{1,0:T(8,128)(2,1)S(1)}, u32[]{:S(2)}, u32[]{:S(2)}) collective-permute-start(bf16[32,6272]{1,0:T(8,128)(2,1)S(1)} %get-tuple-element.29), channel_id=1, source_target_pairs={{0,2},{1,3},{2,0},{3,1},{4,6},{5,7},{6,4},{7,5},{8,10},{9,11},{10,... | collective-permute-start | bytes 1204232 | tf_op jit(solution)/shard_map/ppermute | solution.py:41
  23.3 12.2 %collective-permute-start.7 = (bf16[32,6272]{1,0:T(8,128)(2,1)S(1)}, bf16[32,6272]{1,0:T(8,128)(2,1)S(1)}, u32[]{:S(2)}, u32[]{:S(2)}) collective-permute-start(bf16[32,6272]{1,0:T(8,128)(2,1)S(1)} %get-tuple-element.29), channel_id=1, source_target_pairs={{0,16},{1,17},{2,18},{3,19},{4,20},{5,21},{6,22},{7,23},{8,9},{9,8... | collective-permute-start | bytes 1204232 | tf_op jit(solution)/shard_map/ppermute | solution.py:41
  24.7 10.7 %collective-permute-start.4 = (bf16[32,6272]{1,0:T(8,128)(2,1)S(1)}, bf16[32,6272]{1,0:T(8,128)(2,1)S(1)}, u32[]{:S(2)}, u32[]{:S(2)}) collective-permute-start(bf16[32,6272]{1,0:T(8,128)(2,1)S(1)} %pad_maximum_fusion.2), channel_id=1, source_target_pairs={{0,16},{1,17},{2,18},{3,19},{4,20},{5,21},{6,22},{7,23},{8,9},{9,8... | collective-permute-start | bytes 1204232 | tf_op jit(solution)/shard_map/ppermute | solution.py:41
  36.7 14.3 %collective-permute-start.10 = (bf16[96,6144]{1,0:T(8,128)(2,1)S(1)}, bf16[96,6144]{1,0:T(8,128)(2,1)S(1)}, u32[]{:S(2)}, u32[]{:S(2)}) collective-permute-start(bf16[96,6144]{1,0:T(8,128)(2,1)S(1)} %get-tuple-element.18), channel_id=1, source_target_pairs={{0,8},{1,9},{2,10},{3,11},{4,12},{5,13},{6,14},{7,15},{8,0},{9,1},... | collective-permute-start | bytes 3538952 | tf_op jit(solution)/shard_map/ppermute | solution.py:41
  36.8 7.9 %collective-permute-start.9 = (bf16[32,6272]{1,0:T(8,128)(2,1)S(1)}, bf16[32,6272]{1,0:T(8,128)(2,1)S(1)}, u32[]{:S(2)}, u32[]{:S(2)}) collective-permute-start(bf16[32,6272]{1,0:T(8,128)(2,1)S(1)} %collective-permute-done.8), channel_id=1, source_target_pairs={{0,16},{1,17},{2,18},{3,19},{4,20},{5,21},{6,22},{7,23},{8,9},{9,8... | collective-permute-start | bytes 1204232 | tf_op jit(solution)/shard_map/ppermute | solution.py:41
  45.4 5.6 %collective-permute-start.11 = (bf16[32,6144]{1,0:T(8,128)(2,1)S(1)}, bf16[32,6144]{1,0:T(8,128)(2,1)S(1)}, u32[]{:S(2)}, u32[]{:S(2)}) collective-permute-start(bf16[32,6144]{1,0:T(8,128)(2,1)S(1)} %get-tuple-element.19), channel_id=1, source_target_pairs={{0,8},{1,9},{2,10},{3,11},{4,12},{5,13},{6,14},{7,15},{8,0},{9,1},... | collective-permute-start | bytes 1179656 | tf_op jit(solution)/shard_map/ppermute | solution.py:41
  45.5 4.6 %copy-start = (bf16[1,6144,1024]{2,1,0:T(8,128)(2,1)S(1)}, bf16[1,6144,1024]{2,1,0:T(8,128)(2,1)}, u32[]{:S(2)}) copy-start(bf16[1,6144,1024]{2,1,0:T(8,128)(2,1)} %source.1) | copy-start | bytes 37748740
  62.3 1.9 %collective-permute-start.18 = (bf16[32,6144]{1,0:T(8,128)(2,1)S(1)}, bf16[32,6144]{1,0:T(8,128)(2,1)S(1)}, u32[]{:S(2)}, u32[]{:S(2)}) collective-permute-start(bf16[32,6144]{1,0:T(8,128)(2,1)S(1)} %get-tuple-element.25), channel_id=1, source_target_pairs={{0,8},{1,9},{2,10},{3,11},{4,12},{5,13},{6,14},{7,15},{8,0},{9,1},... | collective-permute-start | bytes 1179656 | tf_op jit(solution)/shard_map/ppermute | solution.py:41
  65.0 7.8 %collective-permute-start.19 = (bf16[32,6144]{1,0:T(8,128)(2,1)S(1)}, bf16[32,6144]{1,0:T(8,128)(2,1)S(1)}, u32[]{:S(2)}, u32[]{:S(2)}) collective-permute-start(bf16[32,6144]{1,0:T(8,128)(2,1)S(1)} %slice.67), channel_id=1, source_target_pairs={{0,16},{1,17},{2,18},{3,19},{4,20},{5,21},{6,22},{7,23},{8,9},{9,8... | collective-permute-start | bytes 1179656 | tf_op jit(solution)/shard_map/ppermute | solution.py:41
  65.6 8.9 %collective-permute-start.12 = (bf16[96,6144]{1,0:T(8,128)(2,1)S(1)}, bf16[96,6144]{1,0:T(8,128)(2,1)S(1)}, u32[]{:S(2)}, u32[]{:S(2)}) collective-permute-start(bf16[96,6144]{1,0:T(8,128)(2,1)S(1)} %get-tuple-element.21), channel_id=1, source_target_pairs={{0,8},{1,9},{2,10},{3,11},{4,12},{5,13},{6,14},{7,15},{8,0},{9,1},... | collective-permute-start | bytes 3538952 | tf_op jit(solution)/shard_map/ppermute | solution.py:41
  73.0 7.2 %collective-permute-start.20 = (bf16[16,6144]{1,0:T(8,128)(2,1)S(1)}, bf16[16,6144]{1,0:T(8,128)(2,1)S(1)}, u32[]{:S(2)}, u32[]{:S(2)}) collective-permute-start(bf16[16,6144]{1,0:T(8,128)(2,1)S(1)} %slice.69), channel_id=1, source_target_pairs={{0,1},{1,0},{2,3},{3,2},{4,5},{5,4},{6,7},{7,6},{8,24},{9,25},{10,... | collective-permute-start | bytes 589832 | tf_op jit(solution)/shard_map/ppermute | solution.py:41
  76.3 7.7 %collective-permute-start.13 = (bf16[16,6144]{1,0:T(8,128)(2,1)S(1)}, bf16[16,6144]{1,0:T(8,128)(2,1)S(1)}, u32[]{:S(2)}, u32[]{:S(2)}) collective-permute-start(bf16[16,6144]{1,0:T(8,128)(2,1)S(1)} %slice.50), channel_id=1, source_target_pairs={{0,16},{1,17},{2,18},{3,19},{4,20},{5,21},{6,22},{7,23},{8,9},{9,8... | collective-permute-start | bytes 589832 | tf_op jit(solution)/shard_map/ppermute | solution.py:41
  80.2 21.2 %collective-permute-start.21 = (bf16[16,6144]{1,0:T(8,128)(2,1)S(1)}, bf16[16,6144]{1,0:T(8,128)(2,1)S(1)}, u32[]{:S(2)}, u32[]{:S(2)}) collective-permute-start(bf16[16,6144]{1,0:T(8,128)(2,1)S(1)} %slice_add_fusion.4), channel_id=1, source_target_pairs={{0,2},{1,3},{2,0},{3,1},{4,6},{5,7},{6,4},{7,5},{8,10},{9,11},{10,... | collective-permute-start | bytes 589832 | tf_op jit(solution)/shard_map/ppermute | solution.py:41
  81.9 9.7 %collective-permute-start.23 = (bf16[32,6144]{1,0:T(8,128)(2,1)S(1)}, bf16[32,6144]{1,0:T(8,128)(2,1)S(1)}, u32[]{:S(2)}, u32[]{:S(2)}) collective-permute-start(bf16[32,6144]{1,0:T(8,128)(2,1)S(1)} %slice.61), channel_id=1, source_target_pairs={{0,16},{1,17},{2,18},{3,19},{4,20},{5,21},{6,22},{7,23},{8,9},{9,8... | collective-permute-start | bytes 1179656 | tf_op jit(solution)/shard_map/ppermute | solution.py:41
  82.0 16.0 %collective-permute-start.16 = (bf16[32,6144]{1,0:T(8,128)(2,1)S(1)}, bf16[32,6144]{1,0:T(8,128)(2,1)S(1)}, u32[]{:S(2)}, u32[]{:S(2)}) collective-permute-start(bf16[32,6144]{1,0:T(8,128)(2,1)S(1)} %slice.53), channel_id=1, source_target_pairs={{0,16},{1,17},{2,18},{3,19},{4,20},{5,21},{6,22},{7,23},{8,9},{9,8... | collective-permute-start | bytes 1179656 | tf_op jit(solution)/shard_map/ppermute | solution.py:41
  84.0 23.5 %collective-permute-start.14 = (bf16[16,6144]{1,0:T(8,128)(2,1)S(1)}, bf16[16,6144]{1,0:T(8,128)(2,1)S(1)}, u32[]{:S(2)}, u32[]{:S(2)}) collective-permute-start(bf16[16,6144]{1,0:T(8,128)(2,1)S(1)} %get-tuple-element.27), channel_id=1, source_target_pairs={{0,1},{1,0},{2,3},{3,2},{4,5},{5,4},{6,7},{7,6},{8,24},{9,25},{10,... | collective-permute-start | bytes 589832 | tf_op jit(solution)/shard_map/ppermute | solution.py:41
  85.4 22.1 %collective-permute-start.15 = (bf16[16,6144]{1,0:T(8,128)(2,1)S(1)}, bf16[16,6144]{1,0:T(8,128)(2,1)S(1)}, u32[]{:S(2)}, u32[]{:S(2)}) collective-permute-start(bf16[16,6144]{1,0:T(8,128)(2,1)S(1)} %get-tuple-element.28), channel_id=1, source_target_pairs={{0,16},{1,17},{2,18},{3,19},{4,20},{5,21},{6,22},{7,23},{8,9},{9,8... | collective-permute-start | bytes 589832 | tf_op jit(solution)/shard_map/ppermute | solution.py:41
  91.6 7.9 %collective-permute-start.24 = (bf16[16,6144]{1,0:T(8,128)(2,1)S(1)}, bf16[16,6144]{1,0:T(8,128)(2,1)S(1)}, u32[]{:S(2)}, u32[]{:S(2)}) collective-permute-start(bf16[16,6144]{1,0:T(8,128)(2,1)S(1)} %slice.71), channel_id=1, source_target_pairs={{0,1},{1,0},{2,3},{3,2},{4,5},{5,4},{6,7},{7,6},{8,24},{9,25},{10,... | collective-permute-start | bytes 589832 | tf_op jit(solution)/shard_map/ppermute | solution.py:41
  98.0 5.7 %collective-permute-start.17 = (bf16[16,6144]{1,0:T(8,128)(2,1)S(1)}, bf16[16,6144]{1,0:T(8,128)(2,1)S(1)}, u32[]{:S(2)}, u32[]{:S(2)}) collective-permute-start(bf16[16,6144]{1,0:T(8,128)(2,1)S(1)} %slice.65), channel_id=1, source_target_pairs={{0,1},{1,0},{2,3},{3,2},{4,5},{5,4},{6,7},{7,6},{8,24},{9,25},{10,... | collective-permute-start | bytes 589832 | tf_op jit(solution)/shard_map/ppermute | solution.py:41
  99.5 8.0 %collective-permute-start.25 = (bf16[16,6144]{1,0:T(8,128)(2,1)S(1)}, bf16[16,6144]{1,0:T(8,128)(2,1)S(1)}, u32[]{:S(2)}, u32[]{:S(2)}) collective-permute-start(bf16[16,6144]{1,0:T(8,128)(2,1)S(1)} %slice_add_fusion.3), channel_id=1, source_target_pairs={{0,2},{1,3},{2,0},{3,1},{4,6},{5,7},{6,4},{7,5},{8,10},{9,11},{10,... | collective-permute-start | bytes 589832 | tf_op jit(solution)/shard_map/ppermute | solution.py:41
  103.8 9.5 %collective-permute-start.22 = (bf16[16,6144]{1,0:T(8,128)(2,1)S(1)}, bf16[16,6144]{1,0:T(8,128)(2,1)S(1)}, u32[]{:S(2)}, u32[]{:S(2)}) collective-permute-start(bf16[16,6144]{1,0:T(8,128)(2,1)S(1)} %fusion), channel_id=1, source_target_pairs={{0,4},{1,5},{2,6},{3,7},{4,0},{5,1},{6,2},{7,3},{8,12},{9,13},{10,... | collective-permute-start | bytes 589832 | tf_op jit(solution)/shard_map/ppermute | solution.py:41
